TPU v7x, 32 devices: a whole 2x2x4 slice. The times are simulated.
32 devices in a mesh: tp: 4 (over z), dp: 8 (over y, x, core).
Axes of the slice: x: 2, y: 2, z: 4, core: 2. Of those that a mesh axis runs over, the one named last changes fastest.
Arguments:
- w_query: bfloat16 [1024, 1024], P(('dp', 'tp'))
- b_query: bfloat16 [1024], P(('dp', 'tp'))
- w_key: bfloat16 [1024, 1024], P(('dp', 'tp'))
- b_key: bfloat16 [1024], P(('dp', 'tp'))
- w_value: bfloat16 [1024, 1024], P(('dp', 'tp'))
- b_value: bfloat16 [1024], P(('dp', 'tp'))
- w_out: bfloat16 [1024, 1024], P(('dp', 'tp'))
- w_gate: bfloat16 [2816, 1024], P(('dp', 'tp'))
- w_up: bfloat16 [2816, 1024], P(('dp', 'tp'))
- w_down: bfloat16 [1024, 2816], P(('dp', 'tp'))
- gain_attn: bfloat16 [1024], P(('dp', 'tp'))
- gain_mlp: bfloat16 [1024], P(('dp', 'tp'))
- hidden: bfloat16 [2048, 1024], P('dp')
- k_cache: bfloat16 [2048, 64, 16, 64], P('dp', None, 'tp')
- v_cache: bfloat16 [2048, 64, 16, 64], P('dp', None, 'tp')
- lengths: int32 [2048], P('dp')
Outputs:
- output 1: bfloat16 [1024, 1024], P('tp')
- output 2: bfloat16 [1024], P('tp')
- output 3: bfloat16 [1024, 1024], P('tp')
- output 4: bfloat16 [1024], P('tp')
- output 5: bfloat16 [1024, 1024], P('tp')
- output 6: bfloat16 [1024], P('tp')
- output 7: bfloat16 [1024, 1024], P(None, 'tp')
- output 8: bfloat16 [2816, 1024], P('tp')
- output 9: bfloat16 [2816, 1024], P('tp')
- output 10: bfloat16 [1024, 2816], P(None, 'tp')
- output 11: bfloat16 [1024], replicated
- output 12: bfloat16 [1024], replicated
- output 13: bfloat16 [2048, 1024], P('dp')
- output 14: bfloat16 [2048, 64, 16, 64], P('dp', None, 'tp')
- output 15: bfloat16 [2048, 64, 16, 64], P('dp', None, 'tp')
All inputs are finite; a program needn't handle non-finite values.
Results may differ from a plain program's by a relative error of at most 0.013719.
Values are sent between devices in bfloat16 or wider.
A program may use at most 1 GiB of HBM per device.

v0:
```python
import jax
import jax.numpy as jnp
from jax import lax
from jax.sharding import PartitionSpec as P

EPS = 1e-6
THETA = 1000000.0


def rms_scale(act_rows, gain_vec):
    rows_f32 = act_rows.astype(jnp.float32)
    inv_rms = lax.rsqrt(jnp.mean(rows_f32 * rows_f32, axis=-1, keepdims=True) + EPS)
    return (rows_f32 * inv_rms * gain_vec.astype(jnp.float32)).astype(jnp.bfloat16)


def project(act_rows, weight, bias_vec):
    result = jnp.einsum("bd,nd->bn", act_rows, weight, preferred_element_type=jnp.float32)
    return (result + bias_vec.astype(jnp.float32)).astype(jnp.bfloat16)


def rotary(vectors, positions):
    head_dim = vectors.shape[-1]
    half_dim = head_dim // 2
    inv_freq = 1.0 / (THETA ** (jnp.arange(0, head_dim, 2, dtype=jnp.float32) / head_dim))
    angles = positions.astype(jnp.float32)[:, None] * inv_freq[None, :]
    cosine = jnp.cos(angles)[:, None, :]
    sine_tab = jnp.sin(angles)[:, None, :]
    vectors_f32 = vectors.astype(jnp.float32)
    first_half = vectors_f32[..., :half_dim]
    second_half = vectors_f32[..., half_dim:]
    return jnp.concatenate([first_half * cosine - second_half * sine_tab, second_half * cosine + first_half * sine_tab], axis=-1).astype(jnp.bfloat16)


def decode_step(synced, hidden, k_cache, v_cache, lengths):
    w_query, b_query, w_key, b_key, w_value, b_value, w_out, w_gate, w_up, w_down, gain_attn, gain_mlp = synced
    roll_count, cache_len, kv_local, head_dim = k_cache.shape
    q_local = w_query.shape[0] // head_dim
    normed = rms_scale(hidden, gain_attn)
    query_rot = rotary(project(normed, w_query, b_query).reshape(roll_count, q_local, head_dim), lengths)
    key_rot = rotary(project(normed, w_key, b_key).reshape(roll_count, kv_local, head_dim), lengths)
    value_new = project(normed, w_value, b_value).reshape(roll_count, kv_local, head_dim)
    slot_ids = jnp.arange(cache_len)
    at_slot = (slot_ids[None, :] == lengths[:, None])[:, :, None, None]
    k_cache_new = jnp.where(at_slot, key_rot[:, None], k_cache)
    v_cache_new = jnp.where(at_slot, value_new[:, None], v_cache)
    grouped = query_rot.reshape(roll_count, kv_local, q_local // kv_local, head_dim)
    scores = jnp.einsum("bkgd,bskd->bkgs", grouped, k_cache_new, preferred_element_type=jnp.float32) * head_dim ** -0.5
    visible = (slot_ids[None, :] <= lengths[:, None])[:, None, None, :]
    attn_probs = jax.nn.softmax(jnp.where(visible, scores, -1e30), axis=-1).astype(jnp.bfloat16)
    attended = jnp.einsum("bkgs,bskd->bkgd", attn_probs, v_cache_new, preferred_element_type=jnp.float32).astype(jnp.bfloat16).reshape(roll_count, q_local * head_dim)
    attn_part = jnp.einsum("bn,dn->bd", attended, w_out, preferred_element_type=jnp.float32).astype(jnp.bfloat16)
    attn_sum = lax.psum(attn_part, "tp")
    mid_hidden = (hidden.astype(jnp.float32) + attn_sum.astype(jnp.float32)).astype(jnp.bfloat16)
    normed_mlp = rms_scale(mid_hidden, gain_mlp)
    gate_val = jnp.einsum("bd,fd->bf", normed_mlp, w_gate, preferred_element_type=jnp.float32).astype(jnp.bfloat16)
    up_val = jnp.einsum("bd,fd->bf", normed_mlp, w_up, preferred_element_type=jnp.float32).astype(jnp.bfloat16)
    gated = (jax.nn.silu(gate_val.astype(jnp.float32)) * up_val.astype(jnp.float32)).astype(jnp.bfloat16)
    down_part = jnp.einsum("bf,df->bd", gated, w_down, preferred_element_type=jnp.float32).astype(jnp.bfloat16)
    down_sum = lax.psum(down_part, "tp")
    hidden_out = (mid_hidden.astype(jnp.float32) + down_sum.astype(jnp.float32)).astype(jnp.bfloat16)
    return (hidden_out, k_cache_new, v_cache_new)


def solution(mesh):
    dp_size = mesh.shape["dp"]
    tp_size = mesh.shape["tp"]

    def head_rows(block):
        gathered = lax.all_gather(block, "dp", axis=0, tiled=False)
        grouped = gathered.reshape((tp_size, dp_size // tp_size) + block.shape)
        swapped = lax.all_to_all(grouped, "tp", 0, 0, tiled=True)
        return jnp.swapaxes(swapped, 0, 1).reshape((dp_size * block.shape[0],) + block.shape[1:])

    def column_share(block):
        swapped = lax.all_to_all(block, "tp", 1, 0, tiled=True)
        return lax.all_gather(swapped, "dp", axis=0, tiled=True)

    def kv_rows(block, head_dim):
        rank_rows = head_rows(block)
        kv_heads = rank_rows.shape[0] * tp_size // head_dim
        if kv_heads >= tp_size:
            return rank_rows
        whole_rows = lax.all_gather(rank_rows, "tp", axis=0, tiled=True)
        start_row = (lax.axis_index("tp") // (tp_size // kv_heads)) * head_dim
        return lax.dynamic_slice_in_dim(whole_rows, start_row, head_dim, axis=0)

    def whole_vector(block):
        return lax.all_gather(block, ("dp", "tp"), axis=0, tiled=True)

    def local_step(w_query, b_query, w_key, b_key, w_value, b_value, w_out, w_gate, w_up, w_down, gain_attn, gain_mlp, hidden, k_cache, v_cache, lengths):
        head_dim = k_cache.shape[-1]
        synced = (head_rows(w_query), head_rows(b_query),
                  kv_rows(w_key, head_dim), kv_rows(b_key, head_dim),
                  kv_rows(w_value, head_dim), kv_rows(b_value, head_dim),
                  column_share(w_out), head_rows(w_gate), head_rows(w_up), column_share(w_down),
                  whole_vector(gain_attn), whole_vector(gain_mlp))
        return synced + decode_step(synced, hidden, k_cache, v_cache, lengths)

    row_spec = P(("dp", "tp"), None)
    flat_spec = P(("dp", "tp"))
    cache_spec = P("dp", None, "tp", None)
    in_specs = (row_spec, flat_spec, row_spec, flat_spec, row_spec, flat_spec, row_spec, row_spec, row_spec, row_spec, flat_spec, flat_spec, P("dp", None), cache_spec, cache_spec, P("dp"))
    out_specs = (P("tp", None), P("tp"), P("tp", None), P("tp"), P("tp", None), P("tp"), P(None, "tp"), P("tp", None), P("tp", None), P(None, "tp"), P(None), P(None), P("dp", None), cache_spec, cache_spec)
    return jax.shard_map(local_step, mesh=mesh, in_specs=in_specs, out_specs=out_specs, check_vma=False)
```

profile of v0, /device:TPU:0, one launch (start us, length us, event | category | flops | bytes accessed | tf_op | source)
XLA Modules:
  0.0 334.8 jit_solution(14701914762977336413)
XLA Ops:
  13.2 15.2 %all-reduce.6 = (bf16[256]{0:T(256)(128)(2,1)S(1)}, bf16[256]{0:T(256)(128)(2,1)S(1)}, bf16[256]{0:T(256)(128)(2,1)S(1)}) all-reduce(bf16[256]{0:T(256)(128)(2,1)S(1)} %dynamic-update-slice, bf16[256]{0:T(256)(128)(2,1)S(1)} %dynamic-update-slice.1, bf16[256]{0:T(256)(128)(2,1)S(1)} %dynamic-update-slice.2), channel_id=3, replica_groups=mesh['tp'=4,'dp'=8] {'dp'}, use_global_device_ids=true, to_apply=%add | all-reduce | flops 768 | bytes 3072
  29.1 4.9 %all-to-all-start.1 = ((bf16[4,2,32]{2,1,0:T(2,128)(2,1)}), bf16[4,2,32]{2,1,0:T(2,128)(2,1)S(1)}, u32[]{:S(2)}, u32[]{:S(2)}) async-start(bf16[4,2,32]{2,1,0:T(2,128)(2,1)} %reshape.263), calls=%async_computation.1 | async-start | bytes 4096 | tf_op jit(solution)/shard_map/all_to_all | solution.py:71
  34.6 4.7 %all-to-all-done.1 = bf16[4,2,32]{2,1,0:T(2,128)(2,1)S(1)} async-done(((bf16[4,2,32]{2,1,0:T(2,128)(2,1)}), bf16[4,2,32]{2,1,0:T(2,128)(2,1)S(1)}, u32[]{:S(2)}, u32[]{:S(2)}) %all-to-all-start.1) | async-done | bytes 544 | tf_op jit(solution)/shard_map/all_to_all | solution.py:71
  43.2 4.7 %all-to-all-done.3 = bf16[4,2,32]{2,1,0:T(2,128)(2,1)S(1)} async-done(((bf16[4,2,32]{2,1,0:T(2,128)(2,1)}), bf16[4,2,32]{2,1,0:T(2,128)(2,1)S(1)}, u32[]{:S(2)}, u32[]{:S(2)}) %all-to-all-start.3) | async-done | bytes 544 | tf_op jit(solution)/shard_map/all_to_all | solution.py:71
  52.6 3.9 %all-to-all-done.5 = bf16[4,2,32]{2,1,0:T(2,128)(2,1)S(1)} async-done(((bf16[4,2,32]{2,1,0:T(2,128)(2,1)}), bf16[4,2,32]{2,1,0:T(2,128)(2,1)S(1)}, u32[]{:S(2)}, u32[]{:S(2)}) %all-to-all-start.5) | async-done | bytes 544 | tf_op jit(solution)/shard_map/all_to_all | solution.py:71
  59.8 10.0 %all-gather = bf16[256,1024]{1,0:T(8,128)(2,1)} all-gather(bf16[32,1024]{1,0:T(8,128)(2,1)} %param.16), channel_id=2, replica_groups=mesh['tp'=4,'dp'=8] {'dp'}, dimensions={0}, use_global_device_ids=true | all-gather | bytes 589824 | tf_op jit(solution)/shard_map/all_gather | solution.py:69
  69.7 5.2 %all-to-all-start = ((bf16[4,2,32,1024]{3,2,1,0:T(8,128)(2,1)}), bf16[4,2,32,1024]{3,2,1,0:T(8,128)(2,1)S(1)}, u32[]{:S(2)}, u32[]{:S(2)}) async-start(bf16[4,2,32,1024]{3,2,1,0:T(8,128)(2,1)} %bitcast.2), calls=%async_computation | async-start | bytes 1048576 | tf_op jit(solution)/shard_map/all_to_all | solution.py:71
  79.3 39.8 %all-reduce.5 = (bf16[1024]{0:T(1024)(128)(2,1)S(1)}, bf16[1024]{0:T(1024)(128)(2,1)}) all-reduce(bf16[1024]{0:T(1024)(128)(2,1)S(1)} %dynamic-update-slice.3, bf16[1024]{0:T(1024)(128)(2,1)S(1)} %dynamic-update-slice.4), channel_id=1, replica_groups=mesh['tp'=4,'dp'=8] {'dp','tp'}, use_global_device_ids=true, to_apply=%add.3 | all-reduce | flops 2048 | bytes 8192
  122.2 10.9 %all-gather.2 = bf16[256,1024]{1,0:T(8,128)(2,1)} all-gather(bf16[32,1024]{1,0:T(8,128)(2,1)} %param.18), channel_id=4, replica_groups=mesh['tp'=4,'dp'=8] {'dp'}, dimensions={0}, use_global_device_ids=true | all-gather | bytes 589824 | tf_op jit(solution)/shard_map/all_gather | solution.py:69
  133.1 10.1 %all-gather.4 = bf16[256,1024]{1,0:T(8,128)(2,1)} all-gather(bf16[32,1024]{1,0:T(8,128)(2,1)} %param.20), channel_id=6, replica_groups=mesh['tp'=4,'dp'=8] {'dp'}, dimensions={0}, use_global_device_ids=true | all-gather | bytes 589824 | tf_op jit(solution)/shard_map/all_gather | solution.py:69
  144.0 3.7 %all-to-all-start.2 = ((bf16[4,2,32,1024]{3,2,1,0:T(8,128)(2,1)}), bf16[4,2,32,1024]{3,2,1,0:T(8,128)(2,1)S(1)}, u32[]{:S(2)}, u32[]{:S(2)}) async-start(bf16[4,2,32,1024]{3,2,1,0:T(8,128)(2,1)} %bitcast.7), calls=%async_computation.2 | async-start | bytes 1048576 | tf_op jit(solution)/shard_map/all_to_all | solution.py:71
  148.8 9.8 %all_gather.72 = bf16[1024,256]{1,0:T(8,128)(2,1)S(1)} all-gather(bf16[128,256]{1,0:T(8,128)(2,1)S(1)} %bitcast.67), channel_id=1, replica_groups=mesh['tp'=4,'dp'=8] {'dp'}, dimensions={0}, use_global_device_ids=true | all-gather | bytes 589824 | tf_op jit(solution)/shard_map/all_gather | solution.py:76
  159.1 3.4 %all-to-all-done.2 = bf16[4,2,32,1024]{3,2,1,0:T(8,128)(2,1)S(1)} async-done(((bf16[4,2,32,1024]{3,2,1,0:T(8,128)(2,1)}), bf16[4,2,32,1024]{3,2,1,0:T(8,128)(2,1)S(1)}, u32[]{:S(2)}, u32[]{:S(2)}) %all-to-all-start.2) | async-done | bytes 524320 | tf_op jit(solution)/shard_map/all_to_all | solution.py:71
  166.8 6.3 %all-to-all-done.9 = bf16[32,4,704]{2,0,1:T(8,128)(2,1)S(1)} async-done(((bf16[32,4,704]{2,0,1:T(8,128)(2,1)}), bf16[32,4,704]{2,0,1:T(8,128)(2,1)S(1)}, u32[]{:S(2)}, u32[]{:S(2)}) %all-to-all-start.9) | async-done | bytes 180256 | tf_op jit(solution)/shard_map/all_to_all | solution.py:75
  173.1 3.7 %all-to-all-start.4 = ((bf16[4,2,32,1024]{3,2,1,0:T(8,128)(2,1)}), bf16[4,2,32,1024]{3,2,1,0:T(8,128)(2,1)S(1)}, u32[]{:S(2)}, u32[]{:S(2)}) async-start(bf16[4,2,32,1024]{3,2,1,0:T(8,128)(2,1)} %bitcast.11), calls=%async_computation.4 | async-start | bytes 1048576 | tf_op jit(solution)/shard_map/all_to_all | solution.py:71
  176.7 12.4 %multiply_reduce_fusion.1 = (f32[256,4,64]{0,1,2:T(4,128)}, bf16[256,64,4,64]{0,3,2,1:T(8,128)(2,1)}) fusion(f32[256,4,64]{0,2,1:T(8,128)S(1)} %get-tuple-element.111, bf16[256,64,4,64]{0,3,2,1:T(8,128)(2,1)} %param.29, bf16[256,4,64]{0,2,1:T(8,128)(2,1)S(1)} %get-tuple-element.112, pred[256,64]{0,1:T(8,128)(4,1)S(1)} %get-tuple-element.110), kind=kLoop, calls=%fused_computation.3 | loop fusion | flops 16711680 | bytes 17448960
  189.2 4.9 %all-to-all-start.7 = ((bf16[4,2,88,1024]{3,2,1,0:T(8,128)(2,1)}), bf16[4,2,88,1024]{3,2,1,0:T(8,128)(2,1)S(1)}, u32[]{:S(2)}, u32[]{:S(2)}) async-start(bf16[4,2,88,1024]{3,2,1,0:T(8,128)(2,1)} %bitcast.53), calls=%async_computation.7 | async-start | bytes 2883584 | tf_op jit(solution)/shard_map/all_to_all | solution.py:71
  196.6 10.9 %multiply_reduce_fusion = (bf16[256,4,64]{0,2,1:T(8,128)(2,1)S(1)}, bf16[256,64,4,64]{0,3,2,1:T(8,128)(2,1)}) fusion(f32[256,4,64]{0,1,2:T(4,128)S(1)} %copy.104, bf16[256,64,4,64]{0,3,2,1:T(8,128)(2,1)} %param.30, bf16[256,4,64]{0,2,1:T(8,128)(2,1)S(1)} %bitcast.68, pred[256,64]{0,1:T(8,128)(4,1)S(1)} %get-tuple-element.110), kind=kLoop, calls=%fused_computation.2 | loop fusion | flops 16711680 | bytes 17317888 | tf_op jit(solution)/shard_map/bkgs,bskd->bkgd/dot_general | solution.py:50
  209.5 24.7 %all-to-all-done.7 = bf16[4,2,88,1024]{3,2,1,0:T(8,128)(2,1)S(1)} async-done(((bf16[4,2,88,1024]{3,2,1,0:T(8,128)(2,1)}), bf16[4,2,88,1024]{3,2,1,0:T(8,128)(2,1)S(1)}, u32[]{:S(2)}, u32[]{:S(2)}) %all-to-all-start.7) | async-done | bytes 1441824 | tf_op jit(solution)/shard_map/all_to_all | solution.py:71
  234.2 3.6 %all-to-all-start.8 = ((bf16[4,2,88,1024]{3,2,1,0:T(8,128)(2,1)}), bf16[4,2,88,1024]{3,2,1,0:T(8,128)(2,1)S(1)}, u32[]{:S(2)}, u32[]{:S(2)}) async-start(bf16[4,2,88,1024]{3,2,1,0:T(8,128)(2,1)} %bitcast.54), calls=%async_computation.8 | async-start | bytes 2883584 | tf_op jit(solution)/shard_map/all_to_all | solution.py:71
  238.0 23.5 %all-reduce.10.cloned.1.call-done = bf16[256,1024]{1,0:T(8,128)(2,1)} async-done(((bf16[256,1024]{1,0:T(8,128)(2,1)}), bf16[256,1024]{1,0:T(8,128)(2,1)}) %all-reduce.10.cloned.1.call-update) | async-done | bytes 524304 | tf_op jit(solution)/shard_map/psum | solution.py:52
  265.0 14.5 %all-to-all-done.8 = bf16[4,2,88,1024]{3,2,1,0:T(8,128)(2,1)S(1)} async-done(((bf16[4,2,88,1024]{3,2,1,0:T(8,128)(2,1)}), bf16[4,2,88,1024]{3,2,1,0:T(8,128)(2,1)S(1)}, u32[]{:S(2)}, u32[]{:S(2)}) %all-to-all-start.8) | async-done | bytes 1441824 | tf_op jit(solution)/shard_map/all_to_all | solution.py:71
  283.0 4.6 %convolution_convert_fusion.1 = bf16[256,1024]{1,0:T(8,128)(2,1)} fusion(bf16[1024,704]{1,0:T(8,128)(2,1)} %all-gather.12.cloned.1.call-done, bf16[704,1024]{1,0:T(8,128)(2,1)} %bitcast.57, f32[256,704]{0,1:T(8,128)S(1)} %fusion.4, bf16[256,1024]{1,0:T(8,128)(2,1)S(1)} %copy-done, f32[1024]{0:T(1024)S(1)} %convert_element_type.135, f32[256]{0:T(256)S(1)} %add_rsqrt_fusion), kind=kOutput, calls=%fused_computation.13 | convolution fusion | flops 740950016 | bytes 4658176 | tf_op jit(solution)/shard_map/bf,df->bd/dot_general | solution.py:58
  289.1 35.7 %all-reduce.12.cloned.1.call-done = bf16[256,1024]{1,0:T(8,128)(2,1)} async-done(((bf16[256,1024]{1,0:T(8,128)(2,1)}), bf16[256,1024]{1,0:T(8,128)(2,1)}) %all-reduce.12.cloned.1.call-update) | async-done | bytes 524304 | tf_op jit(solution)/shard_map/psum | solution.py:59
  (106 shorter events, 47.0 us)
Async XLA Ops:
  8.0 135.4 %copy-start.7 = (s32[256]{0:T(256)S(1)}, s32[256]{0:T(256)}, u32[]{:S(2)}) copy-start(s32[256]{0:T(256)} %param.31) | copy-start | bytes 3076
  8.0 135.2 %copy-start.1 = (bf16[256,1024]{1,0:T(8,128)(2,1)S(1)}, bf16[256,1024]{1,0:T(8,128)(2,1)}, u32[]{:S(2)}) copy-start(bf16[256,1024]{1,0:T(8,128)(2,1)} %param.28) | copy-start | bytes 1572868
  8.0 181.1 %all-gather.14.cloned.1.call-start = ((), (), s32[]{:S(2)}) async-start(), calls=%async_computation.13 | async-start | bytes 1622016 | tf_op jit(solution)/shard_map/all_gather | solution.py:69
  29.1 10.2 %all-to-all-start.1 = ((bf16[4,2,32]{2,1,0:T(2,128)(2,1)}), bf16[4,2,32]{2,1,0:T(2,128)(2,1)S(1)}, u32[]{:S(2)}, u32[]{:S(2)}) async-start(bf16[4,2,32]{2,1,0:T(2,128)(2,1)} %reshape.263), calls=%async_computation.1 | async-start | bytes 4096 | tf_op jit(solution)/shard_map/all_to_all | solution.py:71
  39.3 8.6 %all-to-all-start.3 = ((bf16[4,2,32]{2,1,0:T(2,128)(2,1)}), bf16[4,2,32]{2,1,0:T(2,128)(2,1)S(1)}, u32[]{:S(2)}, u32[]{:S(2)}) async-start(bf16[4,2,32]{2,1,0:T(2,128)(2,1)} %reshape.267), calls=%async_computation.3 | async-start | bytes 4096 | tf_op jit(solution)/shard_map/all_to_all | solution.py:71
  47.9 8.6 %all-to-all-start.5 = ((bf16[4,2,32]{2,1,0:T(2,128)(2,1)}), bf16[4,2,32]{2,1,0:T(2,128)(2,1)S(1)}, u32[]{:S(2)}, u32[]{:S(2)}) async-start(bf16[4,2,32]{2,1,0:T(2,128)(2,1)} %reshape.271), calls=%async_computation.5 | async-start | bytes 4096 | tf_op jit(solution)/shard_map/all_to_all | solution.py:71
  56.5 13.3 %all-to-all-start.6 = ((bf16[32,4,256]{2,0,1:T(8,128)(2,1)}), bf16[32,4,256]{2,0,1:T(8,128)(2,1)S(1)}, u32[]{:S(2)}, u32[]{:S(2)}) async-start(bf16[32,4,256]{2,0,1:T(8,128)(2,1)} %bitcast.52), calls=%async_computation.6 | async-start | bytes 131072 | tf_op jit(solution)/shard_map/all_to_all | solution.py:75
  69.7 74.3 %all-to-all-start = ((bf16[4,2,32,1024]{3,2,1,0:T(8,128)(2,1)}), bf16[4,2,32,1024]{3,2,1,0:T(8,128)(2,1)S(1)}, u32[]{:S(2)}, u32[]{:S(2)}) async-start(bf16[4,2,32,1024]{3,2,1,0:T(8,128)(2,1)} %bitcast.2), calls=%async_computation | async-start | bytes 1048576 | tf_op jit(solution)/shard_map/all_to_all | solution.py:71
  74.9 134.5 %all-gather.16.cloned.1.call-start = ((), (), s32[]{:S(2)}) async-start(), calls=%async_computation.14 | async-start | bytes 1622016 | tf_op jit(solution)/shard_map/all_gather | solution.py:69
  119.7 46.3 %copy-start.8 = (f32[1024]{0:T(1024)}, f32[1024]{0:T(1024)S(1)}, u32[]{:S(2)}) copy-start(f32[1024]{0:T(1024)S(1)} %convert_element_type.116) | copy-start | bytes 12292
  144.0 18.5 %all-to-all-start.2 = ((bf16[4,2,32,1024]{3,2,1,0:T(8,128)(2,1)}), bf16[4,2,32,1024]{3,2,1,0:T(8,128)(2,1)S(1)}, u32[]{:S(2)}, u32[]{:S(2)}) async-start(bf16[4,2,32,1024]{3,2,1,0:T(8,128)(2,1)} %bitcast.7), calls=%async_computation.2 | async-start | bytes 1048576 | tf_op jit(solution)/shard_map/all_to_all | solution.py:71
  147.7 18.7 %copy-start.11 = (f32[256]{0:T(256)}, f32[256]{0:T(256)S(1)}, u32[]{:S(2)}) copy-start(f32[256]{0:T(256)S(1)} %add_rsqrt_fusion.1) | copy-start | bytes 3076
  148.0 17.9 %copy-start.12 = (bf16[256]{0:T(256)(128)(2,1)}, bf16[256]{0:T(256)(128)(2,1)S(1)}, u32[]{:S(2)}) copy-start(bf16[256]{0:T(256)(128)(2,1)S(1)} %reshape.264) | copy-start | bytes 1540
  148.1 17.8 %copy-start.13 = (bf16[256]{0:T(256)(128)(2,1)}, bf16[256]{0:T(256)(128)(2,1)S(1)}, u32[]{:S(2)}) copy-start(bf16[256]{0:T(256)(128)(2,1)S(1)} %reshape.268) | copy-start | bytes 1540
  148.2 17.7 %copy-start.14 = (bf16[256]{0:T(256)(128)(2,1)}, bf16[256]{0:T(256)(128)(2,1)S(1)}, u32[]{:S(2)}) copy-start(bf16[256]{0:T(256)(128)(2,1)S(1)} %reshape.272) | copy-start | bytes 1540
  162.5 10.6 %all-to-all-start.9 = ((bf16[32,4,704]{2,0,1:T(8,128)(2,1)}), bf16[32,4,704]{2,0,1:T(8,128)(2,1)S(1)}, u32[]{:S(2)}, u32[]{:S(2)}) async-start(bf16[32,4,704]{2,0,1:T(8,128)(2,1)} %copy.88), calls=%async_computation.9 | async-start | bytes 393216 | tf_op jit(solution)/shard_map/all_to_all | solution.py:75
  173.1 16.1 %all-to-all-start.4 = ((bf16[4,2,32,1024]{3,2,1,0:T(8,128)(2,1)}), bf16[4,2,32,1024]{3,2,1,0:T(8,128)(2,1)S(1)}, u32[]{:S(2)}, u32[]{:S(2)}) async-start(bf16[4,2,32,1024]{3,2,1,0:T(8,128)(2,1)} %bitcast.11), calls=%async_computation.4 | async-start | bytes 1048576 | tf_op jit(solution)/shard_map/all_to_all | solution.py:71
  189.2 45.0 %all-to-all-start.7 = ((bf16[4,2,88,1024]{3,2,1,0:T(8,128)(2,1)}), bf16[4,2,88,1024]{3,2,1,0:T(8,128)(2,1)S(1)}, u32[]{:S(2)}, u32[]{:S(2)}) async-start(bf16[4,2,88,1024]{3,2,1,0:T(8,128)(2,1)} %bitcast.53), calls=%async_computation.7 | async-start | bytes 2883584 | tf_op jit(solution)/shard_map/all_to_all | solution.py:71
  194.0 67.5 %all-reduce.10.cloned.1.call-start = ((), (), s32[]{:S(2)}) async-start(), calls=%async_computation.11 | async-start | bytes 1048576 | tf_op jit(solution)/shard_map/psum | solution.py:52
  207.6 30.4 %copy-start.10 = (bf16[1024]{0:T(1024)(128)(2,1)S(1)}, bf16[1024]{0:T(1024)(128)(2,1)}, u32[]{:S(2)}) copy-start(bf16[1024]{0:T(1024)(128)(2,1)} %get-tuple-element.139) | copy-start | bytes 6148
  208.7 74.2 %all-gather.12.cloned.1.call-start = ((), (), s32[]{:S(2)}) async-start(), calls=%async_computation.10 | async-start | bytes 1769472 | tf_op jit(solution)/shard_map/all_gather | solution.py:76
  234.2 45.3 %all-to-all-start.8 = ((bf16[4,2,88,1024]{3,2,1,0:T(8,128)(2,1)}), bf16[4,2,88,1024]{3,2,1,0:T(8,128)(2,1)S(1)}, u32[]{:S(2)}, u32[]{:S(2)}) async-start(bf16[4,2,88,1024]{3,2,1,0:T(8,128)(2,1)} %bitcast.54), calls=%async_computation.8 | async-start | bytes 2883584 | tf_op jit(solution)/shard_map/all_to_all | solution.py:71
  237.7 87.1 %all-reduce.12.cloned.1.call-start = ((), (), s32[]{:S(2)}) async-start(), calls=%async_computation.12 | async-start | bytes 1048576 | tf_op jit(solution)/shard_map/psum | solution.py:59
  265.0 18.0 %copy-start = (bf16[256,1024]{1,0:T(8,128)(2,1)S(1)}, bf16[256,1024]{1,0:T(8,128)(2,1)}, u32[]{:S(2)}) copy-start(bf16[256,1024]{1,0:T(8,128)(2,1)} %get-tuple-element.96) | copy-start | bytes 1572868
  (6 other events, 37.8 us)
Sparse Core Ops, SparseCore 0:
  10.7 27.5 all-gather.13
  77.6 25.3 all-gather.15
  212.0 25.7 all-gather.11
Sparse Core Ops, SparseCore 1:
  208.8 52.6 all-reduce.9
  287.6 37.1 all-reduce.11
where the time goes:
time: 336 us; the launch traced here: 335 us
  waiting for transfers between devices  124 us (37%)
  blocking collectives  95.7 us (28%)
  starting transfers between devices  39.3 us (12%)
  other arithmetic  31.1 us (9%)
  local copies, waits for them, and re-layouts  18.3 us (5%)
  between operations  16.9 us (5%)
  matrix products  10 us (3%)
    all_to_all x8, waiting for transfers between devices, head_rows(): swapped = lax.all_to_all(grouped, 'tp', 0, 0, tiled=True)  55.9 us
    unnamed x2, blocking collectives  55 us
    psum x1, waiting for transfers between devices, decode_step(): down_sum = lax.psum(down_part, 'tp')  35.7 us
    all_to_all x8, starting transfers between devices, head_rows(): swapped = lax.all_to_all(grouped, 'tp', 0, 0, tiled=True)  32.3 us
    all_gather x3, blocking collectives, head_rows(): gathered = lax.all_gather(block, 'dp', axis=0, tiled=False)  31 us
    psum x1, waiting for transfers between devices, decode_step(): attn_sum = lax.psum(attn_part, 'tp')  23.5 us
    unnamed x2, other arithmetic  12.4 us
    dot_general x1, other arithmetic, decode_step(): jnp.einsum('bkgs,bskd->bkgd', attn_probs, v_cache_new, preferred_element_...  10.9 us
  transfers between devices with their start and end apart: 15, of which 9 were waited for; matrix products, arithmetic and copies ran while one was open for 15% of the time, Pallas kernels for 0%

commit v1 on v0

v1 whole, which is shorter than its diff:
```python
import functools
import math

import jax
import jax.numpy as jnp
from jax import lax
from jax.experimental import pallas as pl
from jax.experimental.pallas import tpu as pltpu
from jax.sharding import PartitionSpec as P

EPS = 1e-6
THETA = 1000000.0
MESH = pl.DeviceIdType.MESH
BF16, F32 = jnp.bfloat16, jnp.float32
TP, DP = 4, 8
PEERS = TP * DP - 1
HEAD, HALF = 64, 32
WIDTH, QUARTER, LANES = 1024, 256, 128
BLOCK, WIDE_BLOCK = 32, 88
FF, FF_PAD = 704, 768
MIB = 2**20


def _place():
    z, dp = lax.axis_index("tp"), lax.axis_index("dp")
    core, col = dp % 2, dp // 2
    x, y = col % 2, col // 2
    cols = (col, col + 1 - 2 * x, col + 2 - 4 * y, 3 - col)
    peers = {"x": dp + 2 - 4 * x, "y": dp + 4 - 8 * y, "d": dp + 1 - 2 * core}
    return z, dp, core, col, cols, peers


def _remote(src, dst, send, recv, tp, dp):
    return pltpu.make_async_remote_copy(
        src_ref=src, dst_ref=dst, send_sem=send, recv_sem=recv, device_id={"tp": tp, "dp": dp}, device_id_type=MESH
    )


def _rows(start, size):
    return pl.ds(pl.multiple_of(start, 8), size)


def _lanes(start, size):
    return pl.ds(pl.multiple_of(start, 128), size)


def _signal(sem, tp, dp):
    pl.semaphore_signal(sem, inc=1, device_id={"tp": tp, "dp": dp}, device_id_type=MESH)


def _dot(a, b, ca, cb):
    return lax.dot_general(a, b, (((ca,), (cb,)), ((), ())), preferred_element_type=F32)


def _iota(shape, axis):
    return lax.broadcasted_iota(jnp.int32, shape, axis)


def _sublane(shape):
    return _iota(shape, 0)


def _lane(shape):
    return _iota(shape, 1)


def _in_hbm(array):
    return pltpu.with_memory_space_constraint(array, pltpu.HBM)


def _rms(act, gain_row):
    act = act.astype(F32)
    inv = lax.rsqrt(jnp.mean(act * act, axis=-1, keepdims=True) + EPS)
    return (act * inv * gain_row).astype(BF16)


class _Spread:
    def __init__(self, tp, dp, cols, peers, src_own, region, halves, total, send, recv):
        self.tp, self.cols, self.peers = tp, cols, peers
        self.src_own, self.region, self.halves, self.total = src_own, region, halves, total
        self.send, self.recv = send, recv
        self.sent = []

    def _go(self, src, dst, peer, recv_index):
        copy = _remote(src, dst, self.send.at[len(self.sent)], self.recv.at[recv_index], self.tp, self.peers[peer])
        copy.start()
        self.sent.append(copy)

    def _got(self, ref, recv_index):
        _remote(ref, ref, self.send.at[0], self.recv.at[recv_index], self.tp, self.peers["x"]).wait_recv()

    def first(self):
        own = self.region(self.cols[0])
        self._go(self.src_own, own, "x", 0)
        self._go(self.src_own, own, "y", 1)
        self._go(self.src_own, own, "d", 4)

    def second(self):
        at_x, at_y = self.region(self.cols[1]), self.region(self.cols[2])
        self._got(at_x, 0)
        upper = self.halves(self.cols[1], 0)
        self._go(upper, upper, "y", 2)
        self._go(at_x, at_x, "d", 4)
        self._got(at_y, 1)
        lower = self.halves(self.cols[2], 1)
        self._go(lower, lower, "x", 3)
        self._go(at_y, at_y, "d", 4)

    def third(self):
        upper, lower = self.halves(self.cols[3], 0), self.halves(self.cols[3], 1)
        self._got(upper, 2)
        self._go(upper, upper, "d", 4)
        self._got(lower, 3)
        self._go(lower, lower, "d", 4)

    def last(self):
        self._got(self.total, 4)

    def drain(self):
        for copy in self.sent:
            copy.wait_send()


SPREAD_SENDS, SPREAD_RECVS = 9, 5
Q, K, V, OUT, DOWN, GATE, UP = range(7)
ROW_SHARED = (Q, K, V, GATE, UP)


def _gather_kernel(
    wq, wk, wv, wo, wd, wg, wu, bq, bk, bv, ga, gm, hid, lens, kc, vc,
    oq, ok, ov, oo, rd, rg, ru, qt, kt, vt, obq, obk, obv, oga, ogm, hid_v, kc_v, vc_v,
    sq, sk, sv, so, sd, sg, su, tq, tk, tv, tg, tu, dcut, vecs, lens_v, aux, board, act,
    load_sem, vec_sem, own_sem, s0_send, s0_recv, s1_send, s1_recv, sp_send, sp_recv, aux_send, aux_recv,
):
    z, dp, core, col, cols, peers = _place()
    device = dp * TP + z
    own_here = z == col
    away = jnp.logical_not(own_here)
    at_peer = (dp, peers["x"], peers["y"], 2 * cols[3] + core)
    hbm = (wq, wk, wv, wo, wd, wg, wu)
    source = (sq, sk, sv, so, sd, sg, su)
    staged = {Q: tq, K: tk, V: tv, GATE: tg, UP: tu}

    loads = [pltpu.make_async_copy(src, dst, load_sem.at[i]) for i, (src, dst) in enumerate(
        zip(hbm + (hid, lens, kc, vc), source + (hid_v, lens_v, kc_v, vc_v)))]
    small = [pltpu.make_async_copy(src, vecs.at[i], vec_sem.at[i]) for i, src in enumerate((bq, bk, bv, ga, gm))]
    for copy in loads[:GATE + 2] + small + loads[GATE + 2:]:
        copy.start()

    barrier = pltpu.get_barrier_semaphore()

    @pl.loop(1, TP * DP)
    def _(k):
        other = (device + k) % (TP * DP)
        _signal(barrier, other % TP, other // TP)

    for copy in small:
        copy.wait()
    spots = [(_lane((BLOCK, LANES)) == _sublane((BLOCK, LANES)) + BLOCK * r).astype(BF16) for r in range(TP)]
    aux[0] = sum(_dot(vecs[r], spot, 1, 0) for r, spot in enumerate(spots))
    aux[1] = _dot(vecs[TP], spots[0], 1, 0)
    board[pl.ds(device, 1)] = aux[...].reshape(1, 2, 1, LANES)
    loads[DOWN].wait()
    for t in range(TP):
        dcut[t, :, :FF] = sd[:, FF * t:FF * (t + 1)]
        dcut[t, :, FF:] = jnp.zeros((BLOCK, FF_PAD - FF), BF16)
    for w in (Q, K, V, OUT, GATE, UP):
        loads[w].wait()

    pl.semaphore_wait(barrier, PEERS)

    sent = []
    guarded = []

    def lanes_of(column):
        return _lanes(column * QUARTER, QUARTER)

    def root(w, plane_row):
        rows = source[w].shape[0]
        if w in (GATE, UP):
            return lambda column: (rg if w == GATE else ru).at[_rows(plane_row * rows, rows), :]
        ref = (oq, ok, ov)[w]
        return lambda column: ref.at[_rows((core * TP + plane_row) * rows, rows), lanes_of(column)]

    def scatter(w):
        for m in (1, 2, 3):
            src = source[w].at[:, lanes_of(cols[m])]
            sems = s0_send.at[w, m], s0_recv.at[w, m], z, at_peer[m]
            landing = _remote(src, root(w, z)(cols[m]), *sems)
            passing = _remote(src, staged[w].at[m], *sems)

            @pl.when(own_here)
            def _():
                landing.start()

            @pl.when(away)
            def _():
                passing.start()
            sent.append(passing)

        @pl.when(own_here)
        def _():
            pltpu.make_async_copy(hbm[w].at[:, lanes_of(col)], root(w, z)(col), own_sem.at[w]).start()

    def forward(w):
        for m in range(4):
            piece = source[w].at[:, lanes_of(col)] if m == 0 else staged[w].at[m]
            copy = _remote(piece, root(w, z)(col), s1_send.at[w, m], s1_recv.at[w], cols[m], dp)
            if m:
                _remote(staged[w].at[m], staged[w].at[m], s0_send.at[w, m], s0_recv.at[w, m], z, dp).wait_recv()
            elsewhere = cols[m] != z

            @pl.when(elsewhere)
            def _():
                copy.start()
            guarded.append((elsewhere, copy))

    def got_root(w):
        ref = (oq, ok, ov, None, None, rg, ru)[w]
        rows = source[w].shape[0]
        _remote(ref.at[pl.ds(0, 3 * rows), pl.ds(0, QUARTER)], ref.at[pl.ds(0, 3 * rows), pl.ds(0, QUARTER)],
                s1_send.at[w, 0], s1_recv.at[w], z, peers["x"]).wait_recv()

        @pl.when(own_here)
        def _():
            pltpu.make_async_copy(hbm[w].at[:, lanes_of(col)], root(w, z)(col), own_sem.at[w]).wait()

    def columns(w, piece, dst):
        for m in (1, 2, 3):
            plane = (z + m) % TP
            copy = _remote(piece(plane), dst, s1_send.at[w, m], s1_recv.at[w], plane, dp)
            copy.start()
            sent.append(copy)

    def got_columns(w, ref):
        _remote(ref.at[pl.ds(0, 3 * BLOCK)], ref.at[pl.ds(0, 3 * BLOCK)], s1_send.at[w, 0], s1_recv.at[w], z,
                peers["x"]).wait_recv()

    for w in (Q, K, V):
        scatter(w)
    out_rows = oo.at[_rows(dp * LANES + z * BLOCK, BLOCK), :]
    out_own = pltpu.make_async_copy(wo.at[:, lanes_of(z)], out_rows, own_sem.at[OUT])
    out_own.start()
    columns(OUT, lambda plane: so.at[:, lanes_of(plane)], out_rows)

    def announce(k):
        other = (device + k) % (TP * DP)
        return _remote(aux, board.at[device], aux_send, aux_recv, other % TP, other // TP)

    @pl.loop(1, TP * DP)
    def _(k):
        announce(k).start()

    for w in (GATE, UP):
        scatter(w)

    def qkv_spread(w, ref):
        return _Spread(
            z, dp, cols, peers,
            ref.at[_rows(core * LANES, LANES), lanes_of(col)],
            lambda column: ref.at[_rows(core * LANES, LANES), lanes_of(column)],
            lambda column, half: ref.at[_rows(core * LANES + HEAD * half, HEAD), lanes_of(column)],
            ref.at[_rows((1 - core) * LANES, LANES), :],
            sp_send.at[w], sp_recv.at[w])

    spreads = [qkv_spread(Q, oq), qkv_spread(K, ok), qkv_spread(V, ov)]
    spreads.append(_Spread(
        z, dp, cols, peers,
        oo.at[_rows(dp * LANES, LANES), :],
        lambda column: oo.at[_rows((2 * column + core) * LANES, LANES), :],
        lambda column, half: oo.at[_rows((2 * column + core) * LANES + HEAD * half, HEAD), :],
        oo.at[pl.ds(0, WIDTH // 2), :],
        sp_send.at[OUT], sp_recv.at[OUT]))

    for w in (Q, K, V):
        forward(w)
    down_rows = rd.at[_rows(z * BLOCK, BLOCK), :]
    columns(DOWN, lambda plane: dcut.at[plane], down_rows)
    down_rows[...] = dcut[z]
    for w in (GATE, UP):
        forward(w)

    for w in (Q, K, V):
        got_root(w)
        spreads[w].first()
    spreads[Q].second()
    spreads[K].second()
    got_columns(OUT, oo)
    out_own.wait()
    spreads[OUT].first()
    spreads[Q].third()
    spreads[V].second()
    spreads[K].third()

    landed = board.at[pl.ds(0, PEERS)]
    _remote(landed, landed, aux_send, aux_recv, z, peers["x"]).wait_recv()
    sub = _sublane((BLOCK, LANES))
    first, second = jnp.zeros((BLOCK, LANES), F32), jnp.zeros((BLOCK, LANES), F32)
    for i in range(TP * DP):
        first = jnp.where(sub == i, board[i, 0], first)
        second = jnp.where(sub == i, board[i, 1], second)
    first, second = first.astype(BF16), second.astype(BF16)

    def spread_row(table, offset, count, keep):
        width = count * BLOCK
        spot = (_sublane((LANES, width)) == _lane((LANES, width)) % BLOCK + offset).astype(BF16)
        wide = _dot(table, spot, 1, 0)
        mine = _sublane((BLOCK, width)) == keep + _lane((BLOCK, width)) // BLOCK
        return jnp.sum(jnp.where(mine, wide, 0.0), axis=0, keepdims=True)

    gain_row = spread_row(first, 3 * BLOCK, TP * DP, 0)
    oga[...] = gain_row.astype(BF16)
    ogm[...] = spread_row(second, 0, TP * DP, 0).astype(BF16)
    for r, ref in enumerate((obq, obk, obv)):
        ref[...] = spread_row(first, BLOCK * r, DP, DP * z).astype(BF16)

    def bias_column(r):
        tall_shape = (QUARTER, BLOCK)
        pick = (_lane(tall_shape) == DP * z + _sublane(tall_shape) // BLOCK).astype(BF16)
        tall = _dot(pick, first, 1, 0)
        mine = _lane(tall.shape) == BLOCK * r + _sublane(tall.shape) % BLOCK
        return jnp.sum(jnp.where(mine, tall, 0.0), axis=1, keepdims=True)

    for copy in loads[UP + 1:UP + 3]:
        copy.wait()
    act[...] = _rms(hid_v[...], gain_row)

    inv_freq = jnp.exp(_sublane((HALF, QUARTER)).astype(F32) * (-math.log(THETA) / HALF))
    angle = lens_v[...].astype(F32) * inv_freq
    cosine, sine = jnp.cos(angle), jnp.sin(angle)

    def project(weight, r):
        return (_dot(weight[...], act[...], 1, 1) + bias_column(r)).astype(BF16)

    def rotate(vec, out):
        vec = vec.astype(F32)
        for h in range(TP):
            base = HEAD * h
            lo, hi = vec[base:base + HALF], vec[base + HALF:base + HEAD]
            out[base:base + HALF] = (lo * cosine - hi * sine).astype(BF16)
            out[base + HALF:base + HEAD] = (hi * cosine + lo * sine).astype(BF16)

    spreads[V].third()
    spreads[Q].last()
    rotate(project(oq, Q), qt)
    spreads[K].last()
    rotate(project(ok, K), kt)
    spreads[V].last()
    vt[...] = project(ov, V)

    spreads[OUT].second()
    spreads[OUT].third()
    spreads[OUT].last()
    got_columns(DOWN, rd)
    got_root(GATE)
    got_root(UP)

    for copy in loads[UP + 3:]:
        copy.wait()
    for copy in sent:
        copy.wait_send()
    for elsewhere, copy in guarded:
        @pl.when(elsewhere)
        def _():
            copy.wait_send()
    for spread in spreads:
        spread.drain()
    _remote(landed, landed, aux_send, aux_recv, z, peers["x"]).wait_send()


def _gather(weights, vectors, hid, lens, kc, vc):
    vmem = pl.BlockSpec(memory_space=pltpu.VMEM)
    anywhere = pl.BlockSpec(memory_space=pltpu.HBM)
    sizes = [(QUARTER, WIDTH)] * 3 + [(WIDTH, QUARTER), (LANES, FF_PAD)] + [(TP * WIDE_BLOCK, QUARTER)] * 2
    sizes += [(QUARTER, QUARTER)] * 3 + [(1, QUARTER)] * 3 + [(1, WIDTH)] * 2 + [hid.shape, kc.shape, vc.shape]
    dma = pltpu.SemaphoreType.DMA
    inputs = [_in_hbm(a) for a in (*weights, *vectors, hid, lens, kc, vc)]
    return pl.pallas_call(
        _gather_kernel,
        out_shape=[pltpu.VMEM(size, BF16) for size in sizes],
        in_specs=[anywhere] * len(inputs),
        out_specs=[vmem] * len(sizes),
        scratch_shapes=[pltpu.VMEM(w.shape, BF16) for w in weights]
        + [pltpu.VMEM((4, weights[w].shape[0], QUARTER), BF16) for w in ROW_SHARED] + [
            pltpu.VMEM((TP, BLOCK, FF_PAD), BF16), pltpu.VMEM((5, 1, BLOCK), BF16), pltpu.VMEM(lens.shape, jnp.int32),
            pltpu.VMEM((2, 1, LANES), F32), pltpu.VMEM((TP * DP, 2, 1, LANES), F32), pltpu.VMEM(hid.shape, BF16),
            dma((11,)), dma((5,)), dma((7,)), dma((7, 4)), dma((7, 4)), dma((7, 4)), dma((7,)),
            dma((4, SPREAD_SENDS)), dma((4, SPREAD_RECVS)), dma, dma],
        compiler_params=pltpu.CompilerParams(collective_id=0, has_side_effects=True, vmem_limit_bytes=16 * MIB),
        cost_estimate=pl.CostEstimate(flops=2 * 10**10, bytes_accessed=MIB, transcendentals=0),
        name="gather",
    )(*inputs)


SLOTS = 8
BUFFERS = 3


def _attend_kernel(
    kc, vc, qt, kn, vn, lens, wq, wk, wv, wo, bq, bk, bv, ga, gm,
    ko, vo, out, oq, ok, ov, oo, obq, obk, obv, oga, ogm,
    stage, score, total, qf, sem, pass_sem,
):
    count = kc.shape[0] // SLOTS
    passing = [pltpu.make_async_copy(src, dst, pass_sem.at[i])
               for i, (src, dst) in enumerate(((wq, oq), (wk, ok), (wv, ov), (wo, oo)))]
    for copy in passing:
        copy.start()
    for src, dst in ((bq, obq), (bk, obk), (bv, obv), (ga, oga), (gm, ogm)):
        dst[...] = src[...].reshape(dst.shape)
    qf[...] = qt[...].astype(F32)
    lens_row = lens[...]
    lens_b = lens_row.astype(F32).astype(BF16)

    def put(dst, index, chunk):
        return pltpu.make_async_copy(stage.at[index], dst.at[pl.ds(chunk * SLOTS, SLOTS)], sem.at[index])

    def scores(chunk, index):
        for h in range(TP):
            query = qf[HEAD * h:HEAD * (h + 1)]
            fresh = kn[HEAD * h:HEAD * (h + 1)]
            parts = []
            for i in range(SLOTS):
                slot = chunk * SLOTS + i
                here = lens_b == slot.astype(F32).astype(BF16)
                keys = jnp.where(here, fresh, kc[slot, h])
                stage[index, i, h] = keys
                parts.append(jnp.sum(keys.astype(F32) * query, axis=0, keepdims=True))
            score[h, pl.ds(pl.multiple_of(chunk * SLOTS, SLOTS), SLOTS)] = jnp.concatenate(parts, axis=0)

    def values(chunk, index):
        for h in range(TP):
            fresh = vn[HEAD * h:HEAD * (h + 1)]
            weights = score[h, pl.ds(pl.multiple_of(chunk * SLOTS, SLOTS), SLOTS)]
            acc = total[HEAD * h:HEAD * (h + 1)]
            for i in range(SLOTS):
                slot = chunk * SLOTS + i
                here = lens_b == slot.astype(F32).astype(BF16)
                vals = jnp.where(here, fresh, vc[slot, h])
                stage[index, i, h] = vals
                acc = acc + vals.astype(F32) * weights[i:i + 1]
            total[HEAD * h:HEAD * (h + 1)] = acc

    def run(body, dst, first):
        @pl.loop(0, count)
        def _(chunk):
            index = (chunk + first) % BUFFERS

            @pl.when(chunk + first >= BUFFERS)
            def _():
                put(dst, index, 0).wait()

            body(chunk, index)
            put(dst, index, chunk).start()

    run(scores, ko, 0)
    visible = _iota((kc.shape[0], QUARTER), 0) <= lens_row
    for h in range(TP):
        raw = jnp.where(visible, score[h] * (HEAD ** -0.5), -1e30)
        top = jnp.max(raw, axis=0, keepdims=True)
        weight = jnp.exp(raw - top)
        score[h] = (weight / jnp.sum(weight, axis=0, keepdims=True)).astype(BF16).astype(F32)
    total[...] = jnp.zeros_like(total)
    run(values, vo, count)
    out[...] = total[...].T.astype(BF16)
    for index in range(BUFFERS):
        put(vo, index, 0).wait()
    for copy in passing:
        copy.wait()


def _attend(kc, vc, qt, kn, vn, lens, weights, vectors):
    hbm, vmem = pl.BlockSpec(memory_space=pltpu.HBM), pl.BlockSpec(memory_space=pltpu.VMEM)
    return pl.pallas_call(
        _attend_kernel,
        out_shape=[jax.ShapeDtypeStruct(kc.shape, BF16), jax.ShapeDtypeStruct(vc.shape, BF16),
                   jax.ShapeDtypeStruct((QUARTER, QUARTER), BF16)]
        + [jax.ShapeDtypeStruct(w.shape, BF16) for w in weights]
        + [jax.ShapeDtypeStruct((v.size,), BF16) for v in vectors],
        in_specs=[vmem] * 15,
        out_specs=[hbm, hbm, vmem] + [hbm] * 4 + [vmem] * 5,
        scratch_shapes=[pltpu.VMEM((BUFFERS, SLOTS) + kc.shape[1:], BF16), pltpu.VMEM((TP, kc.shape[0], QUARTER), F32),
                        pltpu.VMEM((QUARTER, QUARTER), F32), pltpu.VMEM((QUARTER, QUARTER), F32),
                        pltpu.SemaphoreType.DMA((BUFFERS,)), pltpu.SemaphoreType.DMA((4,))],
        compiler_params=pltpu.CompilerParams(vmem_limit_bytes=14 * MIB),
        cost_estimate=pl.CostEstimate(flops=10**10, bytes_accessed=32 * MIB, transcendentals=0),
        name="attend",
    )(kc, vc, qt, kn, vn, lens, *weights, *vectors)


ROOT = TP * WIDE_BLOCK
CHUNK = 32
CHUNKS = QUARTER // CHUNK
LAG = 2


class _LineSum:
    def __init__(self, part, inbox, mid, cross, send, recv):
        self.part, self.inbox, self.mid, self.cross, self.send, self.recv = part, inbox, mid, cross, send, recv
        z, dp = lax.axis_index("tp"), lax.axis_index("dp")
        self.pair, self.across, self.dp = z + 1 - 2 * (z % 2), 3 - z, dp
        self.inner = jnp.logical_and(z >= 1, z <= 2)

    def rows(self, k):
        return pl.ds(k * CHUNK, CHUNK)

    def to_pair(self, ref, k):
        return _remote(ref.at[self.rows(k)], self.inbox.at[self.rows(k)], self.send.at[0, k], self.recv.at[0, k],
                       self.pair, self.dp)

    def to_across(self, k):
        return _remote(self.mid.at[self.rows(k)], self.cross.at[self.rows(k)], self.send.at[1, k], self.recv.at[1, k],
                       self.across, self.dp)

    def push(self, k):
        @pl.when(jnp.logical_not(self.inner))
        def _():
            self.to_pair(self.part, k).start()

    def join(self, k):
        @pl.when(self.inner)
        def _():
            rows = self.rows(k)
            self.to_pair(self.part, k).wait_recv()
            self.mid[rows] = (self.part[rows].astype(F32) + self.inbox[rows].astype(F32)).astype(BF16)
            self.to_across(k).start()

    def finish(self, k):
        rows = self.rows(k)

        @pl.when(self.inner)
        def _():
            self.to_across(k).wait_recv()
            self.part[rows] = (self.mid[rows].astype(F32) + self.cross[rows].astype(F32)).astype(BF16)
            self.to_pair(self.part, k).start()

        @pl.when(jnp.logical_not(self.inner))
        def _():
            self.to_pair(self.part, k).wait_recv()
            self.to_pair(self.part, k).wait_send()
            self.part[rows] = self.inbox[rows]

    def drain(self):
        @pl.when(self.inner)
        def _():
            for k in range(CHUNKS):
                self.to_pair(self.part, k).wait_send()
                self.to_across(k).wait_send()


def _mlp_kernel(
    o, wo, hid, rg, ru, rd, gain,
    out, og, ou, od,
    part, inbox, mid, cross, part2, inbox2, mid2, cross2, x1, norm, down,
    send1, recv1, send2, recv2, sp_send, sp_recv,
):
    z, dp, core, col, cols, peers = _place()

    barrier = pltpu.get_barrier_semaphore()
    pair, across = z + 1 - 2 * (z % 2), 3 - z
    inner = jnp.logical_and(z >= 1, z <= 2)
    _signal(barrier, pair, dp)
    for peer in ("x", "y", "d"):
        _signal(barrier, z, peers[peer])

    @pl.when(inner)
    def _():
        _signal(barrier, across, dp)

    part[...] = _dot(o[...], wo[...], 1, 1).astype(BF16)

    def rows_spread(w, root, ref):
        return _Spread(
            z, dp, cols, peers, root,
            lambda column: ref.at[_rows(core * ROOT, ROOT), _lanes(column * QUARTER, QUARTER)],
            lambda column, half: ref.at[_rows(core * ROOT + 176 * half, 176), _lanes(column * QUARTER, QUARTER)],
            ref.at[_rows((1 - core) * ROOT, ROOT), :],
            sp_send.at[w], sp_recv.at[w])

    spreads = [rows_spread(0, rg, og), rows_spread(1, ru, ou)]
    spreads.append(_Spread(
        z, dp, cols, peers, rd,
        lambda column: down.at[_rows((2 * column + core) * LANES, LANES), :],
        lambda column, half: down.at[_rows((2 * column + core) * LANES + HEAD * half, HEAD), :],
        down.at[pl.ds(0, 512), :],
        sp_send.at[2], sp_recv.at[2]))
    og[_rows(core * ROOT, ROOT), _lanes(col * QUARTER, QUARTER)] = rg[...]
    ou[_rows(core * ROOT, ROOT), _lanes(col * QUARTER, QUARTER)] = ru[...]
    down[_rows(dp * LANES, LANES), :] = rd[...]

    @pl.when(inner)
    def _():
        pl.semaphore_wait(barrier, 5)

    @pl.when(jnp.logical_not(inner))
    def _():
        pl.semaphore_wait(barrier, 4)

    first = _LineSum(part, inbox, mid, cross, send1, recv1)
    for k in range(CHUNKS):
        first.push(k)
    spreads[0].first()
    spreads[1].first()
    for k in range(CHUNKS):
        first.join(k)
        if k >= LAG:
            first.finish(k - LAG)
        if k == 2:
            spreads[0].second()
            spreads[2].first()
        if k == 5:
            spreads[1].second()
    for k in range(CHUNKS - LAG, CHUNKS):
        first.finish(k)
    spreads[0].third()
    spreads[2].second()
    spreads[1].third()

    x1[...] = (hid[...].astype(F32) + part[...].astype(F32)).astype(BF16)
    norm[...] = _rms(x1[...], gain[...].astype(F32))

    spreads[2].third()
    for spread in spreads:
        spread.last()
    od[...] = down[...].T[0:FF]

    second = _LineSum(part2, inbox2, mid2, cross2, send2, recv2)
    for half in range(2):
        rows = pl.ds(LANES * half, LANES)
        gate = _dot(norm[rows], og[...], 1, 1).astype(BF16).astype(F32)
        up = _dot(norm[rows], ou[...], 1, 1).astype(BF16).astype(F32)
        gated = (jax.nn.silu(gate) * up).astype(BF16)
        part2[rows] = _dot(gated, od[...], 1, 0).astype(BF16)
        for k in range(CHUNKS // 2 * half, CHUNKS // 2 * (half + 1)):
            second.push(k)
    for k in range(CHUNKS):
        second.join(k)
        if k >= LAG:
            second.finish(k - LAG)
    for k in range(CHUNKS - LAG, CHUNKS):
        second.finish(k)
    out[...] = (x1[...].astype(F32) + part2[...].astype(F32)).astype(BF16)

    first.drain()
    second.drain()
    for spread in spreads:
        spread.drain()


def _mlp(o, wo, hid, rg, ru, rd, gain):
    vmem = pl.BlockSpec(memory_space=pltpu.VMEM)
    sizes = [(QUARTER, WIDTH), (FF, WIDTH), (FF, WIDTH), (FF, WIDTH)]
    dma = pltpu.SemaphoreType.DMA
    return pl.pallas_call(
        _mlp_kernel,
        out_shape=[pltpu.VMEM(size, BF16) for size in sizes],
        in_specs=[vmem] * 7,
        out_specs=[vmem] * 4,
        scratch_shapes=[pltpu.VMEM((QUARTER, WIDTH), BF16)] * 10 + [pltpu.VMEM((WIDTH, FF_PAD), BF16)] + [
            dma((2, CHUNKS))] * 4 + [dma((3, SPREAD_SENDS)), dma((3, SPREAD_RECVS))],
        compiler_params=pltpu.CompilerParams(collective_id=1, has_side_effects=True, vmem_limit_bytes=24 * MIB),
        cost_estimate=pl.CostEstimate(flops=2 * 10**10, bytes_accessed=MIB, transcendentals=0),
        name="mlp",
    )(o, wo, hid, rg, ru, rd, gain)


def _emit_kernel(*refs):
    count = len(refs) // 2
    copies = [pltpu.make_async_copy(refs[i], refs[count + i], refs[-1].at[i]) for i in range(count)]
    for copy in copies:
        copy.start()
    for copy in copies:
        copy.wait()


def _emit(*arrays):
    vmem, hbm = pl.BlockSpec(memory_space=pltpu.VMEM), pl.BlockSpec(memory_space=pltpu.HBM)
    return pl.pallas_call(
        _emit_kernel,
        out_shape=[jax.ShapeDtypeStruct(a.shape, a.dtype) for a in arrays],
        in_specs=[vmem] * len(arrays),
        out_specs=[hbm] * len(arrays),
        scratch_shapes=[pltpu.SemaphoreType.DMA((len(arrays),))],
        compiler_params=pltpu.CompilerParams(vmem_limit_bytes=4 * MIB),
        name="emit",
    )(*arrays)


def solution(mesh):
    def local_step(wq, bq, wk, bk, wv, bv, wo, wg, wu, wd, ga, gm, hid, k_cache, v_cache, lengths):
        lens = lengths.reshape(1, -1)
        vectors = [v.reshape(1, -1) for v in (bq, bk, bv, ga, gm)]
        kc, vc = jnp.transpose(k_cache, (1, 2, 3, 0)), jnp.transpose(v_cache, (1, 2, 3, 0))
        (gq, gk, gv, go, rd, rg, ru, qt, kt, vt, gbq, gbk, gbv, gga, ggm, hid_v, kc_v, vc_v) = _gather(
            (wq, wk, wv, wo, wd, wg, wu), vectors, hid, lens, kc, vc)
        ko, vo, o, oq, ok, ov, oo, obq, obk, obv, oga, ogm = _attend(
            kc_v, vc_v, qt, kt, vt, lens, (gq, gk, gv, go), (gbq, gbk, gbv, gga, ggm))
        out, og, ou, od = _emit(*_mlp(o, go, hid_v, rg, ru, rd, ggm))
        return (oq, obq, ok, obk, ov, obv, oo, og, ou, od.T, oga, ogm, out,
                jnp.transpose(ko, (3, 0, 1, 2)), jnp.transpose(vo, (3, 0, 1, 2)))

    row_spec = P(("dp", "tp"), None)
    flat_spec = P(("dp", "tp"))
    cache_spec = P("dp", None, "tp", None)
    in_specs = (row_spec, flat_spec, row_spec, flat_spec, row_spec, flat_spec, row_spec, row_spec, row_spec, row_spec,
                flat_spec, flat_spec, P("dp", None), cache_spec, cache_spec, P("dp"))
    out_specs = (P("tp", None), P("tp"), P("tp", None), P("tp"), P("tp", None), P("tp"), P(None, "tp"), P("tp", None),
                 P("tp", None), P(None, "tp"), P(None), P(None), P("dp", None), cache_spec, cache_spec)
    return jax.shard_map(local_step, mesh=mesh, in_specs=in_specs, out_specs=out_specs, check_vma=False)
```

time: 336 us -> 93 us (0.28)
  waiting for transfers between devices: 124 us -> 0 us
  blocking collectives: 95.7 us -> 0 us
  Pallas kernels: 0 us -> 92.2 us
  starting transfers between devices: 39.3 us -> 0 us
  other arithmetic: 31.1 us -> 0 us
  local copies, waits for them, and re-layouts: 18.3 us -> 0.01 us
  between operations: 16.9 us -> 0.69 us
  matrix products: 10 us -> 0 us
    pallas_call x0 -> x4, Pallas kernels: none -> 92.2 us  [the longest x1 47.9 us: _mlp(): pl.pallas_call(_mlp_kernel, out_shape=[pltpu.VMEM(size, BF16) for size in...]
    all_to_all x10 -> x0, waiting for transfers between devices: 62.2 us -> none  [the longest x8 55.9 us: head_rows(): swapped = lax.all_to_all(grouped, 'tp', 0, 0, tiled=True)]
    psum x2 -> x0, waiting for transfers between devices: 59.2 us -> none  [the longest x1 35.7 us: decode_step(): down_sum = lax.psum(down_part, 'tp')]
    unnamed x2 -> x0, blocking collectives: 55 us -> none
    all_gather x4 -> x0, blocking collectives: 40.7 us -> none  [the longest x3 31 us: head_rows(): gathered = lax.all_gather(block, 'dp', axis=0, tiled=False)]
    all_to_all x10 -> x0, starting transfers between devices: 38.9 us -> none  [the longest x8 32.3 us: head_rows(): swapped = lax.all_to_all(grouped, 'tp', 0, 0, tiled=True)]
    unnamed x2 -> x0, other arithmetic: 12.4 us -> none
    dot_general x1 -> x0, other arithmetic: 10.9 us -> none  [decode_step(): jnp.einsum('bkgs,bskd->bkgd', attn_probs, v_cache_new, preferred_element_...]
  transfers between devices with their start and end apart: 15 -> 0, of which waited for: 9 -> 0; matrix products, arithmetic and copies ran while one was open for 15% -> 0% of each run, Pallas kernels for 0% -> 0%
where the time goes in v1:
time: 93 us; the launch traced here: 92.9 us
  Pallas kernels  92.2 us (99%)
    pallas_call x1, Pallas kernels, _mlp(): pl.pallas_call(_mlp_kernel, out_shape=[pltpu.VMEM(size, BF16) for size in...  47.9 us
    pallas_call x1, Pallas kernels, _gather(): pl.pallas_call(_gather_kernel, out_shape=[pltpu.VMEM(size, BF16) for size...  33.6 us
    pallas_call x1, Pallas kernels, _attend(): pl.pallas_call(_attend_kernel, out_shape=[jax.ShapeDtypeStruct(kc.shape,...  8.42 us
    pallas_call x1, Pallas kernels, _emit(): pl.pallas_call(_emit_kernel, out_shape=[jax.ShapeDtypeStruct(a.shape, a.d...  2.26 us

profile of v1, /device:TPU:0, one launch (start us, length us, event | category | flops | bytes accessed | tf_op | source)
XLA Modules:
  0.0 92.9 jit_solution(14529023011493922701)
XLA Ops:
  0.7 0.0 copy-start
  0.7 33.6 %gather.1 = (bf16[256,1024]{1,0:T(8,128)(2,1)S(1)}, bf16[256,1024]{1,0:T(8,128)(2,1)S(1)}, bf16[256,1024]{1,0:T(8,128)(2,1)S(1)}, bf16[1024,256]{1,0:T(8,128)(2,...) custom-call(bf16[32,1024]{1,0:T(8,128)(2,1)} %wq.1, ...), custom_call_target="tpu_custom_call" | custom-call | flops 20000000000 | bytes 1048576 | tf_op jit(solution)/shard_map/gather/pallas_call | solution.py:378
  34.3 0.0 copy-done
  34.3 8.4 %attend.1 = (bf16[64,4,64,256]{3,2,1,0:T(8,128)(2,1)}, bf16[64,4,64,256]{3,2,1,0:T(8,128)(2,1)}, bf16[256,256]{1,0:T(8,128)(2,1)S(1)}, bf16[256,1024]{1,0:T(8,12...) custom-call(bf16[64,4,64,256]{3,2,1,0:T(8,128)(2,1)S(1)} %get-tuple-, ...), custom_call_target="tpu_custom_call" | custom-call | flops 10000000000 | bytes 33554432 | tf_op jit(solution)/shard_map/attend/pallas_call | solution.py:474
  42.7 47.9 %mlp.1 = (bf16[256,1024]{1,0:T(8,128)(2,1)S(1)}, bf16[704,1024]{1,0:T(8,128)(2,1)S(1)}, bf16[704,1024]{1,0:T(8,128)(2,1)S(1)}, bf16[704,1024]{1,0:T(8,128)(2,1)S(1)}) custom-call(bf16[256,256]{1,0:T(8,128)(2,1)S(1)} %get-tuple-element.74.o, bf16[1024,256]{1,0:T(8,128)(2,1)S(1)} %get-tuple-element.61.wo, bf16[256,1024]{1,0:T(8,128)(2,1)S(1)} %get-tuple-element.75.hid, ...), custom_call_target="tpu_custom_call" | custom-call | flops 20000000000 | bytes 1048576 | tf_op jit(solution)/shard_map/mlp/pallas_call | solution.py:654
  90.6 2.3 %emit.1 = (bf16[256,1024]{1,0:T(8,128)(2,1)}, bf16[704,1024]{1,0:T(8,128)(2,1)}, bf16[704,1024]{1,0:T(8,128)(2,1)}, bf16[704,1024]{1,0:T(8,128)(2,1)}) custom-call(bf16[256,1024]{1,0:T(8,128)(2,1)S(1)} %get-tuple-element.79.refs_0_, bf16[704,1024]{1,0:T(8,128)(2,1)S(1)} %get-tuple-element.80.refs_1_, bf16[704,1024]{1,0:T(8,128)(2,1)S(1)} %get-tuple-element.81.refs_2_, ...), custom_call_target="tpu_custom_call" | custom-call | tf_op jit(solution)/shard_map/emit/pallas_call | solution.py:678
Async XLA Ops:
  0.7 33.6 %copy-start = (s32[256]{0:T(256)S(1)}, s32[256]{0:T(256)}, u32[]{:S(2)}) copy-start(s32[256]{0:T(256)} %param.31) | copy-start | bytes 3076

commit v2 on v1

v2 whole, which is shorter than its diff:
```python
import functools
import math

import jax
import jax.numpy as jnp
from jax import lax
from jax.experimental import pallas as pl
from jax.experimental.pallas import tpu as pltpu
from jax.sharding import PartitionSpec as P

EPS = 1e-6
THETA = 1000000.0
MESH = pl.DeviceIdType.MESH
BF16, F32 = jnp.bfloat16, jnp.float32
TP, DP = 4, 8
PEERS = TP * DP - 1
HEAD, HALF = 64, 32
WIDTH, QUARTER, LANES = 1024, 256, 128
BLOCK, WIDE_BLOCK = 32, 88
FF, FF_PAD = 704, 768
MIB = 2**20


def _place():
    z, dp = lax.axis_index("tp"), lax.axis_index("dp")
    core, col = dp % 2, dp // 2
    x, y = col % 2, col // 2
    cols = (col, col + 1 - 2 * x, col + 2 - 4 * y, 3 - col)
    peers = {"x": dp + 2 - 4 * x, "y": dp + 4 - 8 * y, "d": dp + 1 - 2 * core}
    return z, dp, core, col, cols, peers


def _remote(src, dst, send, recv, tp, dp):
    return pltpu.make_async_remote_copy(
        src_ref=src, dst_ref=dst, send_sem=send, recv_sem=recv, device_id={"tp": tp, "dp": dp}, device_id_type=MESH
    )


def _rows(start, size):
    return pl.ds(pl.multiple_of(start, 8), size)


def _lanes(start, size):
    return pl.ds(pl.multiple_of(start, 128), size)


def _signal(sem, tp, dp):
    pl.semaphore_signal(sem, inc=1, device_id={"tp": tp, "dp": dp}, device_id_type=MESH)


def _dot(a, b, ca, cb):
    return lax.dot_general(a, b, (((ca,), (cb,)), ((), ())), preferred_element_type=F32)


def _iota(shape, axis):
    return lax.broadcasted_iota(jnp.int32, shape, axis)


def _sublane(shape):
    return _iota(shape, 0)


def _lane(shape):
    return _iota(shape, 1)


def _in_hbm(array):
    return pltpu.with_memory_space_constraint(array, pltpu.HBM)


def _rms(act, gain_row):
    act = act.astype(F32)
    inv = lax.rsqrt(jnp.mean(act * act, axis=-1, keepdims=True) + EPS)
    return (act * inv * gain_row).astype(BF16)


class _Spread:
    def __init__(self, tp, dp, cols, peers, src_own, region, halves, total, send, recv):
        self.tp, self.cols, self.peers = tp, cols, peers
        self.src_own, self.region, self.halves, self.total = src_own, region, halves, total
        self.send, self.recv = send, recv
        self.sent = []

    def _go(self, src, dst, peer, recv_index):
        copy = _remote(src, dst, self.send.at[len(self.sent)], self.recv.at[recv_index], self.tp, self.peers[peer])
        copy.start()
        self.sent.append(copy)

    def _got(self, ref, recv_index):
        _remote(ref, ref, self.send.at[0], self.recv.at[recv_index], self.tp, self.peers["x"]).wait_recv()

    def first(self):
        own = self.region(self.cols[0])
        self._go(self.src_own, own, "x", 0)
        self._go(self.src_own, own, "y", 1)
        self._go(self.src_own, own, "d", 4)

    def second(self):
        at_x, at_y = self.region(self.cols[1]), self.region(self.cols[2])
        self._got(at_x, 0)
        upper = self.halves(self.cols[1], 0)
        self._go(upper, upper, "y", 2)
        self._go(at_x, at_x, "d", 4)
        self._got(at_y, 1)
        lower = self.halves(self.cols[2], 1)
        self._go(lower, lower, "x", 3)
        self._go(at_y, at_y, "d", 4)

    def third(self):
        upper, lower = self.halves(self.cols[3], 0), self.halves(self.cols[3], 1)
        self._got(upper, 2)
        self._go(upper, upper, "d", 4)
        self._got(lower, 3)
        self._go(lower, lower, "d", 4)

    def last(self):
        self._got(self.total, 4)

    def drain(self):
        for copy in self.sent:
            copy.wait_send()


SPREAD_SENDS, SPREAD_RECVS = 9, 5
Q, K, V, OUT, DOWN, GATE, UP = range(7)
ROW_SHARED = (Q, K, V, GATE, UP)
SLOTS = 8
CHUNK = 32
CHUNKS = QUARTER // CHUNK
BLOCK_CHUNKS = 2
LAG = 2


class _LineSum:
    def __init__(self, part, inbox, mid, cross, send, recv, use):
        self.part, self.inbox, self.mid, self.cross, self.send, self.recv = part, inbox, mid, cross, send, recv
        z, dp = lax.axis_index("tp"), lax.axis_index("dp")
        self.pair, self.across, self.dp = z + 1 - 2 * (z % 2), TP - 1 - z, dp
        self.inner = jnp.logical_and(z >= 1, z <= 2)
        self.outer = jnp.logical_not(self.inner)
        self.use = use

    def rows(self, k):
        return pl.ds(k * CHUNK, CHUNK)

    def to_pair(self, k):
        return _remote(self.part.at[self.rows(k)], self.inbox.at[self.rows(k)], self.send.at[0, k],
                       self.recv.at[0, k], self.pair, self.dp)

    def to_across(self, k):
        return _remote(self.mid.at[self.rows(k)], self.cross.at[self.rows(k)], self.send.at[1, k], self.recv.at[1, k],
                       self.across, self.dp)

    def push(self, k):
        @pl.when(self.outer)
        def _():
            self.to_pair(k).start()

    def join(self, k):
        @pl.when(self.inner)
        def _():
            rows = self.rows(k)
            self.to_pair(k).wait_recv()
            self.mid[rows] = (self.part[rows].astype(F32) + self.inbox[rows].astype(F32)).astype(BF16)
            self.to_across(k).start()

    def finish(self, k):
        rows = self.rows(k)

        @pl.when(self.inner)
        def _():
            self.to_across(k).wait_recv()
            total = (self.mid[rows].astype(F32) + self.cross[rows].astype(F32)).astype(BF16)
            self.part[rows] = total
            self.to_pair(k).start()
            self.use(rows, total)

        @pl.when(self.outer)
        def _():
            self.to_pair(k).wait_recv()
            self.use(rows, self.inbox[rows])

    def drain(self):
        for k in range(CHUNKS):
            self.to_pair(k).wait_send()

        @pl.when(self.inner)
        def _():
            for k in range(CHUNKS):
                self.to_across(k).wait_send()


def _step_kernel(
    wq, wk, wv, wo, wd, wg, wu, bq, bk, bv, ga, gm, hid_hbm, lens_hbm, kc_hbm, vc_hbm,
    oq, ok, ov, oo, od, og, ou, kt, vt, obq, obk, obv, oga, ogm, kc, vc, lens, out,
    sq, sk, sv, so, sd, sg, su, tq, tk, tv, tg, tu, dcut, vecs, hid, aux, board, act, qt,
    score, total, attended, part, inbox, mid, cross, part2, inbox2, mid2, cross2, x1,
    load_sem, vec_sem, own_sem, s0_send, s0_recv, s1_send, s1_recv, sp_send, sp_recv, aux_send, aux_recv,
    send1, recv1, send2, recv2,
):
    z, dp, core, col, cols, peers = _place()
    device = dp * TP + z
    own_here = z == col
    away = jnp.logical_not(own_here)
    at_peer = (dp, peers["x"], peers["y"], 2 * cols[3] + core)
    hbm = (wq, wk, wv, wo, wd, wg, wu)
    source = (sq, sk, sv, so, sd, sg, su)
    share = (oq, ok, ov, oo, od, og, ou)
    staged = {Q: tq, K: tk, V: tv, GATE: tg, UP: tu}

    loads = [pltpu.make_async_copy(src, dst, load_sem.at[i]) for i, (src, dst) in enumerate(
        zip(hbm + (hid_hbm, lens_hbm, kc_hbm, vc_hbm), source + (hid, lens, kc, vc)))]
    small = [pltpu.make_async_copy(src, vecs.at[i], vec_sem.at[i]) for i, src in enumerate((bq, bk, bv, ga, gm))]
    for copy in loads[:UP + 1] + small + loads[UP + 1:]:
        copy.start()

    barrier = pltpu.get_barrier_semaphore()

    @pl.loop(1, TP * DP)
    def _(k):
        other = (device + k) % (TP * DP)
        _signal(barrier, other % TP, other // TP)

    for copy in small:
        copy.wait()
    spots = [(_lane((BLOCK, LANES)) == _sublane((BLOCK, LANES)) + BLOCK * r).astype(BF16) for r in range(TP)]
    aux[0] = sum(_dot(vecs[r], spot, 1, 0) for r, spot in enumerate(spots))
    aux[1] = _dot(vecs[TP], spots[0], 1, 0)
    board[pl.ds(device, 1)] = aux[...].reshape(1, 2, 1, LANES)
    for w in (Q, K, V, OUT, GATE, UP):
        loads[w].wait()

    pl.semaphore_wait(barrier, PEERS)

    sent = []
    guarded = []

    def lanes_of(column):
        return _lanes(column * QUARTER, QUARTER)

    def root(w, plane_row):
        rows = source[w].shape[0]
        return lambda column: share[w].at[_rows((core * TP + plane_row) * rows, rows), lanes_of(column)]

    def own_piece(w):
        return pltpu.make_async_copy(hbm[w].at[:, lanes_of(col)], root(w, z)(col), own_sem.at[w])

    def scatter(w):
        for m in (1, 2, 3):
            src = source[w].at[:, lanes_of(cols[m])]
            sems = s0_send.at[w, m], s0_recv.at[w, m], z, at_peer[m]
            landing = _remote(src, root(w, z)(cols[m]), *sems)
            passing = _remote(src, staged[w].at[m], *sems)

            @pl.when(own_here)
            def _():
                landing.start()

            @pl.when(away)
            def _():
                passing.start()
            sent.append(passing)

        @pl.when(own_here)
        def _():
            own_piece(w).start()

    def forward(w):
        for m in range(4):
            piece = source[w].at[:, lanes_of(col)] if m == 0 else staged[w].at[m]
            copy = _remote(piece, root(w, z)(col), s1_send.at[w, m], s1_recv.at[w], cols[m], dp)
            if m:
                _remote(staged[w].at[m], staged[w].at[m], s0_send.at[w, m], s0_recv.at[w, m], z, dp).wait_recv()
            elsewhere = cols[m] != z

            @pl.when(elsewhere)
            def _():
                copy.start()
            guarded.append((elsewhere, copy))

    def columns(w, piece, dst):
        for m in (1, 2, 3):
            plane = (z + m) % TP
            copy = _remote(piece(plane), dst, s1_send.at[w, m], s1_recv.at[w], plane, dp)
            copy.start()
            sent.append(copy)

    def got_root(w):
        rows = source[w].shape[0]
        width = QUARTER if w in ROW_SHARED else share[w].shape[1]
        three = share[w].at[pl.ds(0, 3 * rows), pl.ds(0, width)]
        _remote(three, three, s1_send.at[w, 1], s1_recv.at[w], z, peers["x"]).wait_recv()
        if w in ROW_SHARED:
            @pl.when(own_here)
            def _():
                own_piece(w).wait()

    def rows_spread(w, index):
        ref, size = share[w], TP * source[w].shape[0]
        return _Spread(
            z, dp, cols, peers,
            ref.at[_rows(core * size, size), lanes_of(col)],
            lambda column: ref.at[_rows(core * size, size), lanes_of(column)],
            lambda column, half: ref.at[_rows(core * size + size // 2 * half, size // 2), lanes_of(column)],
            ref.at[_rows((1 - core) * size, size), :],
            sp_send.at[index], sp_recv.at[index])

    def columns_spread(w, index):
        ref = share[w]
        return _Spread(
            z, dp, cols, peers,
            ref.at[_rows(dp * LANES, LANES), :],
            lambda column: ref.at[_rows((2 * column + core) * LANES, LANES), :],
            lambda column, half: ref.at[_rows((2 * column + core) * LANES + HEAD * half, HEAD), :],
            ref.at[pl.ds(0, WIDTH // 2), :],
            sp_send.at[index], sp_recv.at[index])

    spreads = [(rows_spread if w in ROW_SHARED else columns_spread)(w, w) for w in range(7)]

    for w in (Q, K, V):
        scatter(w)
    out_rows = oo.at[_rows(dp * LANES + z * BLOCK, BLOCK), :]
    out_own = pltpu.make_async_copy(wo.at[:, lanes_of(z)], out_rows, own_sem.at[OUT])
    out_own.start()
    columns(OUT, lambda plane: so.at[:, lanes_of(plane)], out_rows)

    def announce(k):
        other = (device + k) % (TP * DP)
        return _remote(aux, board.at[device], aux_send, aux_recv, other % TP, other // TP)

    @pl.loop(1, TP * DP)
    def _(k):
        announce(k).start()

    for w in (GATE, UP):
        scatter(w)
    for w in (Q, K, V):
        forward(w)
    for w in (GATE, UP):
        forward(w)
    loads[DOWN].wait()
    for t in range(TP):
        dcut[t, :, :FF] = sd[:, FF * t:FF * (t + 1)]
        dcut[t, :, FF:] = jnp.zeros((BLOCK, FF_PAD - FF), BF16)
    down_rows = od.at[_rows(dp * LANES + z * BLOCK, BLOCK), :]
    down_rows[...] = dcut[z]
    columns(DOWN, lambda plane: dcut.at[plane], down_rows)

    landed = board.at[pl.ds(0, PEERS)]
    _remote(landed, landed, aux_send, aux_recv, z, peers["x"]).wait_recv()
    sub = _sublane((BLOCK, LANES))
    first, second = jnp.zeros((BLOCK, LANES), F32), jnp.zeros((BLOCK, LANES), F32)
    for i in range(TP * DP):
        first = jnp.where(sub == i, board[i, 0], first)
        second = jnp.where(sub == i, board[i, 1], second)
    first, second = first.astype(BF16), second.astype(BF16)

    def spread_row(table, offset, count, keep):
        width = count * BLOCK
        spot = (_sublane((LANES, width)) == _lane((LANES, width)) % BLOCK + offset).astype(BF16)
        wide = _dot(table, spot, 1, 0)
        mine = _sublane((BLOCK, width)) == keep + _lane((BLOCK, width)) // BLOCK
        return jnp.sum(jnp.where(mine, wide, 0.0), axis=0, keepdims=True)

    gain_row = spread_row(first, 3 * BLOCK, TP * DP, 0)
    gain_mlp = spread_row(second, 0, TP * DP, 0)
    oga[...] = gain_row.astype(BF16)
    ogm[...] = gain_mlp.astype(BF16)
    for r, ref in enumerate((obq, obk, obv)):
        ref[...] = spread_row(first, BLOCK * r, DP, DP * z).astype(BF16)

    def bias_column(r):
        tall_shape = (QUARTER, BLOCK)
        pick = (_lane(tall_shape) == DP * z + _sublane(tall_shape) // BLOCK).astype(BF16)
        tall = _dot(pick, first, 1, 0)
        mine = _lane(tall.shape) == BLOCK * r + _sublane(tall.shape) % BLOCK
        return jnp.sum(jnp.where(mine, tall, 0.0), axis=1, keepdims=True)

    for copy in loads[UP + 1:UP + 3]:
        copy.wait()
    act[...] = _rms(hid[...], gain_row)

    lens_row = lens[...]
    inv_freq = jnp.exp(_sublane((HALF, QUARTER)).astype(F32) * (-math.log(THETA) / HALF))
    angle = lens_row.astype(F32) * inv_freq
    cosine, sine = jnp.cos(angle), jnp.sin(angle)

    for w in (Q, K, V):
        got_root(w)
        spreads[w].first()
    out_own.wait()
    got_root(OUT)
    spreads[OUT].first()
    spreads[Q].second()
    spreads[K].second()
    spreads[V].second()
    spreads[Q].third()
    spreads[OUT].second()
    spreads[K].third()
    spreads[V].third()
    got_root(GATE)
    spreads[GATE].first()

    def project(weight, r):
        return (_dot(weight[...], act[...], 1, 1) + bias_column(r)).astype(BF16)

    def rotate(vec, out):
        vec = vec.astype(F32)
        for h in range(TP):
            base = HEAD * h
            lo, hi = vec[base:base + HALF], vec[base + HALF:base + HEAD]
            out[base:base + HALF] = (lo * cosine - hi * sine).astype(BF16).astype(out.dtype)
            out[base + HALF:base + HEAD] = (hi * cosine + lo * sine).astype(BF16).astype(out.dtype)

    spreads[Q].last()
    rotate(project(oq, Q), qt)
    spreads[K].last()
    rotate(project(ok, K), kt)
    spreads[V].last()
    vt[...] = project(ov, V)
    for copy in loads[UP + 3:]:
        copy.wait()
    spreads[OUT].third()

    def heads(h):
        return slice(HEAD * h, HEAD * (h + 1))

    def chunk_rows(chunk):
        return pl.ds(pl.multiple_of(chunk * SLOTS, SLOTS), SLOTS)

    def scores(start, stop):
        @pl.loop(start, stop)
        def _(chunk):
            for h in range(TP):
                query = qt[heads(h)]
                score[h, chunk_rows(chunk)] = jnp.concatenate([
                    jnp.sum(kc[chunk * SLOTS + i, h].astype(F32) * query, axis=0, keepdims=True)
                    for i in range(SLOTS)], axis=0)

    def values(start, stop):
        @pl.loop(start, stop)
        def _(chunk):
            for h in range(TP):
                weights = score[h, chunk_rows(chunk)]
                acc = total[heads(h)]
                for i in range(SLOTS):
                    acc = acc + vc[chunk * SLOTS + i, h].astype(F32) * weights[i:i + 1]
                total[heads(h)] = acc

    count = kc.shape[0] // SLOTS
    scores(0, count // 2)
    got_root(UP)
    spreads[UP].first()
    scores(count // 2, count)
    spreads[GATE].second()
    slot = _sublane((kc.shape[0], QUARTER))
    for h in range(TP):
        fresh = jnp.sum(kt[heads(h)].astype(F32) * qt[heads(h)], axis=0, keepdims=True)
        raw = jnp.where(slot == lens_row, fresh, score[h]) * (HEAD ** -0.5)
        raw = jnp.where(slot <= lens_row, raw, -1e30)
        weight = jnp.exp(raw - jnp.max(raw, axis=0, keepdims=True))
        weight = (weight / jnp.sum(weight, axis=0, keepdims=True)).astype(BF16).astype(F32)
        newest = jnp.sum(jnp.where(slot == lens_row, weight, 0.0), axis=0, keepdims=True)
        score[h] = jnp.where(slot == lens_row, 0.0, weight)
        total[heads(h)] = vt[heads(h)].astype(F32) * newest
    values(0, count // 2)
    got_root(DOWN)
    spreads[DOWN].first()
    values(count // 2, count)
    attended[...] = total[...].T.astype(BF16)
    spreads[UP].second()
    spreads[OUT].last()

    def after_first(rows, total_rows):
        x1[rows] = (hid[rows].astype(F32) + total_rows.astype(F32)).astype(BF16)

    def after_second(rows, total_rows):
        out[rows] = (x1[rows].astype(F32) + total_rows.astype(F32)).astype(BF16)

    line1 = _LineSum(part, inbox, mid, cross, send1, recv1, after_first)
    line2 = _LineSum(part2, inbox2, mid2, cross2, send2, recv2, after_second)

    for half in range(2):
        rows = pl.ds(LANES * half, LANES)
        part[rows] = _dot(attended[rows], oo[...], 1, 1).astype(BF16)
        for k in range(CHUNKS // 2 * half, CHUNKS // 2 * (half + 1)):
            line1.push(k)
    spreads[GATE].third()
    spreads[DOWN].second()
    spreads[UP].third()

    def mlp(block):
        size = BLOCK_CHUNKS * CHUNK
        rows = pl.ds(block * size, size)
        norm = _rms(x1[rows], gain_mlp)
        gate = _dot(norm, og[...], 1, 1).astype(BF16).astype(F32)
        up = _dot(norm, ou[...], 1, 1).astype(BF16).astype(F32)
        gated = (jax.nn.silu(gate) * up).astype(BF16)
        part2[rows] = _dot(gated, od[:, :FF], 1, 1).astype(BF16)
        for k in range(block * BLOCK_CHUNKS, (block + 1) * BLOCK_CHUNKS):
            line2.push(k)

    def finish_first(k):
        line1.finish(k)
        if k == 1:
            for w in (GATE, UP, DOWN):
                spreads[w].last()
        if (k + 1) % BLOCK_CHUNKS == 0:
            mlp(k // BLOCK_CHUNKS)

    for k in range(CHUNKS):
        line1.join(k)
        if k == LAG:
            spreads[DOWN].third()
        if k >= LAG:
            finish_first(k - LAG)
    for k in range(CHUNKS - LAG, CHUNKS):
        finish_first(k)
    for k in range(CHUNKS):
        line2.join(k)
        if k >= LAG:
            line2.finish(k - LAG)
    for k in range(CHUNKS - LAG, CHUNKS):
        line2.finish(k)

    line1.drain()
    line2.drain()
    for copy in sent:
        copy.wait_send()
    for elsewhere, copy in guarded:
        @pl.when(elsewhere)
        def _():
            copy.wait_send()
    for spread in spreads:
        spread.drain()
    _remote(landed, landed, aux_send, aux_recv, z, peers["x"]).wait_send()


def _step(weights, vectors, hid, lens, kc, vc):
    vmem = pl.BlockSpec(memory_space=pltpu.VMEM)
    anywhere = pl.BlockSpec(memory_space=pltpu.HBM)
    square = (QUARTER, QUARTER)
    sizes = [(QUARTER, WIDTH)] * 3 + [(WIDTH, QUARTER), (WIDTH, FF_PAD)] + [(FF, WIDTH)] * 2
    sizes += [square] * 2 + [(1, QUARTER)] * 3 + [(1, WIDTH)] * 2 + [kc.shape, vc.shape]
    outs = [pltpu.VMEM(size, BF16) for size in sizes] + [pltpu.VMEM(lens.shape, lens.dtype), pltpu.VMEM(hid.shape, BF16)]
    dma = pltpu.SemaphoreType.DMA
    inputs = [_in_hbm(a) for a in (*weights, *vectors, hid, lens, kc, vc)]
    rows = pltpu.VMEM(hid.shape, BF16)
    return pl.pallas_call(
        _step_kernel,
        out_shape=outs,
        in_specs=[anywhere] * len(inputs),
        out_specs=[vmem] * len(outs),
        scratch_shapes=[pltpu.VMEM(w.shape, BF16) for w in weights]
        + [pltpu.VMEM((4, weights[w].shape[0], QUARTER), BF16) for w in ROW_SHARED] + [
            pltpu.VMEM((TP, BLOCK, FF_PAD), BF16), pltpu.VMEM((5, 1, BLOCK), BF16), rows,
            pltpu.VMEM((2, 1, LANES), F32), pltpu.VMEM((TP * DP, 2, 1, LANES), F32), rows, pltpu.VMEM(square, F32),
            pltpu.VMEM((TP, kc.shape[0], QUARTER), F32), pltpu.VMEM(square, F32), pltpu.VMEM(square, BF16)]
        + [rows] * 9 + [
            dma((11,)), dma((5,)), dma((7,)), dma((7, 4)), dma((7, 4)), dma((7, 4)), dma((7,)),
            dma((7, SPREAD_SENDS)), dma((7, SPREAD_RECVS)), dma, dma] + [dma((2, CHUNKS))] * 4,
        compiler_params=pltpu.CompilerParams(collective_id=0, has_side_effects=True, vmem_limit_bytes=24 * MIB),
        cost_estimate=pl.CostEstimate(flops=2 * 10**10, bytes_accessed=MIB, transcendentals=0),
        name="step",
    )(*inputs)


BUFFERS = 4


def _emit_kernel(*refs):
    kc, vc, kn, vn, lens, down = refs[:6]
    plain = refs[6:13]
    vectors = refs[13:18]
    ko, vo, od = refs[18:21]
    plain_out = refs[21:28]
    vectors_out = refs[28:33]
    stage, turned, sem, pass_sem, down_sem = refs[33:]

    passing = [pltpu.make_async_copy(src, dst, pass_sem.at[i]) for i, (src, dst) in enumerate(zip(plain, plain_out))]
    for copy in passing:
        copy.start()
    for src, dst in zip(vectors, vectors_out):
        dst[...] = src[...].reshape(dst.shape)

    lens_b = lens[...].astype(F32).astype(BF16)
    count = kc.shape[0] // SLOTS

    def put(dst, index, chunk):
        return pltpu.make_async_copy(stage.at[index], dst.at[pl.ds(chunk * SLOTS, SLOTS)], sem.at[index])

    def update(old, new, dst, first):
        @pl.loop(0, count)
        def _(chunk):
            index = (chunk + first) % BUFFERS

            @pl.when(chunk + first >= BUFFERS)
            def _():
                put(dst, index, 0).wait()

            for i in range(SLOTS):
                slot = chunk * SLOTS + i
                here = lens_b == slot.astype(F32).astype(BF16)
                for h in range(TP):
                    stage[index, i, h] = jnp.where(here, new[HEAD * h:HEAD * (h + 1)], old[slot, h])
            put(dst, index, chunk).start()

    update(kc, kn, ko, 0)
    turned[...] = down[...].T
    turn = pltpu.make_async_copy(turned.at[pl.ds(0, FF)], od, down_sem)
    turn.start()
    update(vc, vn, vo, count)
    for index in range(BUFFERS):
        put(vo, index, 0).wait()
    for copy in passing + [turn]:
        copy.wait()


def _emit(kc, vc, kn, vn, lens, down, plain, vectors):
    vmem, hbm = pl.BlockSpec(memory_space=pltpu.VMEM), pl.BlockSpec(memory_space=pltpu.HBM)
    shapes = [kc.shape, vc.shape, (FF, WIDTH)] + [a.shape for a in plain] + [(v.size,) for v in vectors]
    dma = pltpu.SemaphoreType.DMA
    return pl.pallas_call(
        _emit_kernel,
        out_shape=[jax.ShapeDtypeStruct(shape, BF16) for shape in shapes],
        in_specs=[vmem] * (6 + len(plain) + len(vectors)),
        out_specs=[hbm] * (3 + len(plain)) + [vmem] * len(vectors),
        scratch_shapes=[pltpu.VMEM((BUFFERS, SLOTS) + kc.shape[1:], BF16), pltpu.VMEM((FF_PAD, WIDTH), BF16),
                        dma((BUFFERS,)), dma((len(plain),)), dma],
        compiler_params=pltpu.CompilerParams(vmem_limit_bytes=12 * MIB),
        cost_estimate=pl.CostEstimate(flops=10**9, bytes_accessed=24 * MIB, transcendentals=0),
        name="emit",
    )(kc, vc, kn, vn, lens, down, *plain, *vectors)


def solution(mesh):
    def local_step(wq, bq, wk, bk, wv, bv, wo, wg, wu, wd, ga, gm, hid, k_cache, v_cache, lengths):
        vectors = [v.reshape(1, -1) for v in (bq, bk, bv, ga, gm)]
        kc, vc = jnp.transpose(k_cache, (1, 2, 3, 0)), jnp.transpose(v_cache, (1, 2, 3, 0))
        (gq, gk, gv, go, gd, gg, gu, kt, vt, gbq, gbk, gbv, gga, ggm, kc_v, vc_v, lens_v, out_v) = _step(
            (wq, wk, wv, wo, wd, wg, wu), vectors, hid, lengths.reshape(1, -1), kc, vc)
        ko, vo, od, oq, ok, ov, oo, og, ou, out, obq, obk, obv, oga, ogm = _emit(
            kc_v, vc_v, kt, vt, lens_v, gd, (gq, gk, gv, go, gg, gu, out_v), (gbq, gbk, gbv, gga, ggm))
        return (oq, obq, ok, obk, ov, obv, oo, og, ou, od.T, oga, ogm, out,
                jnp.transpose(ko, (3, 0, 1, 2)), jnp.transpose(vo, (3, 0, 1, 2)))

    row_spec = P(("dp", "tp"), None)
    flat_spec = P(("dp", "tp"))
    cache_spec = P("dp", None, "tp", None)
    in_specs = (row_spec, flat_spec, row_spec, flat_spec, row_spec, flat_spec, row_spec, row_spec, row_spec, row_spec,
                flat_spec, flat_spec, P("dp", None), cache_spec, cache_spec, P("dp"))
    out_specs = (P("tp", None), P("tp"), P("tp", None), P("tp"), P("tp", None), P("tp"), P(None, "tp"), P("tp", None),
                 P("tp", None), P(None, "tp"), P(None), P(None), P("dp", None), cache_spec, cache_spec)
    return jax.shard_map(local_step, mesh=mesh, in_specs=in_specs, out_specs=out_specs, check_vma=False)
```

time: 93 us -> 86.9 us (0.934)
  Pallas kernels: 92.2 us -> 86 us
    pallas_call x4 -> x2, Pallas kernels: 92.2 us -> 86 us  [the longest x1 77.4 us: _step(): pl.pallas_call(_step_kernel, out_shape=outs, in_specs=[anywhere] * len(in...]
where the time goes in v2:
time: 86.9 us; the launch traced here: 86.7 us
  Pallas kernels  86 us (99%)
    pallas_call x1, Pallas kernels, _step(): pl.pallas_call(_step_kernel, out_shape=outs, in_specs=[anywhere] * len(in...  77.4 us
    pallas_call x1, Pallas kernels, _emit(): pl.pallas_call(_emit_kernel, out_shape=[jax.ShapeDtypeStruct(shape, BF16)...  8.69 us

profile of v2, /device:TPU:0, one launch (start us, length us, event | category | flops | bytes accessed | tf_op | source)
XLA Modules:
  0.0 86.7 jit_solution(13559447031396954574)
XLA Ops:
  0.7 77.4 %step.1 = (bf16[256,1024]{1,0:T(8,128)(2,1)S(1)}, bf16[256,1024]{1,0:T(8,128)(2,1)S(1)}, bf16[256,1024]{1,0:T(8,128)(2,1)S(1)}, bf16[1024,256]{1,0:T(8,128)(2,1)...) custom-call(bf16[32,1024]{1,0:T(8,128)(2,1)} %wq.1, ...), custom_call_target="tpu_custom_call" | custom-call | flops 20000000000 | bytes 1048576 | tf_op jit(solution)/shard_map/step/pallas_call | solution.py:549
  78.0 8.7 %emit.1 = (bf16[64,4,64,256]{3,2,1,0:T(8,128)(2,1)}, bf16[64,4,64,256]{3,2,1,0:T(8,128)(2,1)}, bf16[704,1024]{1,0:T(8,128)(2,1)}, bf16[256,1024]{1,0:T(8,128)(2,...) custom-call(bf16[64,4,64,256]{3,2,1,0:T(8,128)(2,1)S(1)} %get-tuple-, ...), custom_call_target="tpu_custom_call" | custom-call | flops 1000000000 | bytes 25165824 | tf_op jit(solution)/shard_map/emit/pallas_call | solution.py:623

commit v3 on v2

--- a/solution.py
+++ b/solution.py
@@ -1,4 +1,3 @@
-import functools
 import math
 
 import jax
@@ -13,7 +12,6 @@
 MESH = pl.DeviceIdType.MESH
 BF16, F32 = jnp.bfloat16, jnp.float32
 TP, DP = 4, 8
-PEERS = TP * DP - 1
 HEAD, HALF = 64, 32
 WIDTH, QUARTER, LANES = 1024, 256, 128
 BLOCK, WIDE_BLOCK = 32, 88
@@ -192,9 +190,9 @@
 
 def _step_kernel(
     wq, wk, wv, wo, wd, wg, wu, bq, bk, bv, ga, gm, hid_hbm, lens_hbm, kc_hbm, vc_hbm,
-    oq, ok, ov, oo, od, og, ou, kt, vt, obq, obk, obv, oga, ogm, kc, vc, lens, out,
-    sq, sk, sv, so, sd, sg, su, tq, tk, tv, tg, tu, dcut, vecs, hid, aux, board, act, qt,
-    score, total, attended, part, inbox, mid, cross, part2, inbox2, mid2, cross2, x1,
+    oq, ok, ov, oo, od, og, ou, obq, obk, obv, oga, ogm, kc, vc, out,
+    sq, sk, sv, so, sd, sg, su, tq, tk, tv, tg, tu, dcut, vecs, hid, lens, kt, vt, aux, board, act, qt,
+    score, total, down, part, inbox, mid, cross, part2, inbox2, mid2, cross2, x1,
     load_sem, vec_sem, own_sem, s0_send, s0_recv, s1_send, s1_recv, sp_send, sp_recv, aux_send, aux_recv,
     send1, recv1, send2, recv2,
 ):
@@ -205,7 +203,7 @@
     at_peer = (dp, peers["x"], peers["y"], 2 * cols[3] + core)
     hbm = (wq, wk, wv, wo, wd, wg, wu)
     source = (sq, sk, sv, so, sd, sg, su)
-    share = (oq, ok, ov, oo, od, og, ou)
+    share = (oq, ok, ov, oo, down, og, ou)
     staged = {Q: tq, K: tk, V: tv, GATE: tg, UP: tu}
 
     loads = [pltpu.make_async_copy(src, dst, load_sem.at[i]) for i, (src, dst) in enumerate(
@@ -215,22 +213,14 @@
         copy.start()
 
     barrier = pltpu.get_barrier_semaphore()
-
-    @pl.loop(1, TP * DP)
-    def _(k):
-        other = (device + k) % (TP * DP)
-        _signal(barrier, other % TP, other // TP)
-
-    for copy in small:
-        copy.wait()
-    spots = [(_lane((BLOCK, LANES)) == _sublane((BLOCK, LANES)) + BLOCK * r).astype(BF16) for r in range(TP)]
-    aux[0] = sum(_dot(vecs[r], spot, 1, 0) for r, spot in enumerate(spots))
-    aux[1] = _dot(vecs[TP], spots[0], 1, 0)
-    board[pl.ds(device, 1)] = aux[...].reshape(1, 2, 1, LANES)
-    for w in (Q, K, V, OUT, GATE, UP):
+    for peer in (peers["x"], peers["y"], peers["d"], at_peer[3]):
+        _signal(barrier, z, peer)
+    for m in (1, 2, 3):
+        _signal(barrier, (z + m) % TP, dp)
+
+    for w in (Q, K, V):
         loads[w].wait()
-
-    pl.semaphore_wait(barrier, PEERS)
+    pl.semaphore_wait(barrier, 7)
 
     sent = []
     guarded = []
@@ -322,32 +312,63 @@
     out_rows = oo.at[_rows(dp * LANES + z * BLOCK, BLOCK), :]
     out_own = pltpu.make_async_copy(wo.at[:, lanes_of(z)], out_rows, own_sem.at[OUT])
     out_own.start()
+    loads[OUT].wait()
     columns(OUT, lambda plane: so.at[:, lanes_of(plane)], out_rows)
-
-    def announce(k):
-        other = (device + k) % (TP * DP)
-        return _remote(aux, board.at[device], aux_send, aux_recv, other % TP, other // TP)
-
-    @pl.loop(1, TP * DP)
-    def _(k):
-        announce(k).start()
-
     for w in (GATE, UP):
+        loads[w].wait()
         scatter(w)
-    for w in (Q, K, V):
-        forward(w)
-    for w in (GATE, UP):
-        forward(w)
+
+    for copy in small:
+        copy.wait()
+    spots = [(_lane((BLOCK, LANES)) == _sublane((BLOCK, LANES)) + BLOCK * r).astype(BF16) for r in range(TP)]
+    aux[0] = sum(_dot(vecs[r], spot, 1, 0) for r, spot in enumerate(spots))
+    aux[1] = _dot(vecs[TP], spots[0], 1, 0)
+    board[pl.ds(device, 1)] = aux[...].reshape(1, 2, 1, LANES)
+    for m in (1, 2, 3):
+        _remote(aux, board.at[device], aux_send.at[0], aux_recv.at[0], (z + m) % TP, dp).start()
+    y = col // 2
+    steps = ((TP * dp, TP, "d"), (2 * TP * col, 2 * TP, "x"), (4 * TP * y, 4 * TP, "y"))
+
+    def board_got(index, size, sending):
+        part = board.at[pl.ds(0, size)]
+        copy = _remote(part, part, aux_send.at[index], aux_recv.at[index], z, peers["x"])
+        copy.wait_send() if sending else copy.wait_recv()
+
+    def board_step(index):
+        start, size, peer = steps[index]
+        board_got(index, size // 2 if index else 3, False)
+        part = board.at[pl.ds(start, size)]
+        _remote(part, part, aux_send.at[index + 1], aux_recv.at[index + 1], z, peers[peer]).start()
+
     loads[DOWN].wait()
     for t in range(TP):
         dcut[t, :, :FF] = sd[:, FF * t:FF * (t + 1)]
         dcut[t, :, FF:] = jnp.zeros((BLOCK, FF_PAD - FF), BF16)
-    down_rows = od.at[_rows(dp * LANES + z * BLOCK, BLOCK), :]
+    down_rows = down.at[_rows(dp * LANES + z * BLOCK, BLOCK), :]
     down_rows[...] = dcut[z]
+
+    for w in (Q, K, V):
+        forward(w)
+    board_step(0)
     columns(DOWN, lambda plane: dcut.at[plane], down_rows)
-
-    landed = board.at[pl.ds(0, PEERS)]
-    _remote(landed, landed, aux_send, aux_recv, z, peers["x"]).wait_recv()
+    out_own.wait()
+    got_root(OUT)
+    spreads[OUT].first()
+    forward(GATE)
+    board_step(1)
+    got_root(Q)
+    spreads[Q].first()
+    forward(UP)
+    for w in (K, V):
+        got_root(w)
+        spreads[w].first()
+    board_step(2)
+    spreads[Q].second()
+    spreads[OUT].second()
+    spreads[K].second()
+    spreads[V].second()
+    board_got(3, 4 * TP, False)
+
     sub = _sublane((BLOCK, LANES))
     first, second = jnp.zeros((BLOCK, LANES), F32), jnp.zeros((BLOCK, LANES), F32)
     for i in range(TP * DP):
@@ -364,10 +385,10 @@
 
     gain_row = spread_row(first, 3 * BLOCK, TP * DP, 0)
     gain_mlp = spread_row(second, 0, TP * DP, 0)
-    oga[...] = gain_row.astype(BF16)
-    ogm[...] = gain_mlp.astype(BF16)
+    oga[...] = gain_row.astype(BF16).reshape(oga.shape)
+    ogm[...] = gain_mlp.astype(BF16).reshape(ogm.shape)
     for r, ref in enumerate((obq, obk, obv)):
-        ref[...] = spread_row(first, BLOCK * r, DP, DP * z).astype(BF16)
+        ref[...] = spread_row(first, BLOCK * r, DP, DP * z).astype(BF16).reshape(ref.shape)
 
     def bias_column(r):
         tall_shape = (QUARTER, BLOCK)
@@ -385,21 +406,10 @@
     angle = lens_row.astype(F32) * inv_freq
     cosine, sine = jnp.cos(angle), jnp.sin(angle)
 
-    for w in (Q, K, V):
-        got_root(w)
-        spreads[w].first()
-    out_own.wait()
-    got_root(OUT)
-    spreads[OUT].first()
-    spreads[Q].second()
-    spreads[K].second()
-    spreads[V].second()
     spreads[Q].third()
-    spreads[OUT].second()
+    got_root(DOWN)
+    spreads[DOWN].first()
     spreads[K].third()
-    spreads[V].third()
-    got_root(GATE)
-    spreads[GATE].first()
 
     def project(weight, r):
         return (_dot(weight[...], act[...], 1, 1) + bias_column(r)).astype(BF16)
@@ -414,13 +424,13 @@
 
     spreads[Q].last()
     rotate(project(oq, Q), qt)
+    spreads[V].third()
     spreads[K].last()
     rotate(project(ok, K), kt)
-    spreads[V].last()
-    vt[...] = project(ov, V)
+    got_root(GATE)
+    spreads[GATE].first()
     for copy in loads[UP + 3:]:
         copy.wait()
-    spreads[OUT].third()
 
     def heads(h):
         return slice(HEAD * h, HEAD * (h + 1))
@@ -437,57 +447,68 @@
                     jnp.sum(kc[chunk * SLOTS + i, h].astype(F32) * query, axis=0, keepdims=True)
                     for i in range(SLOTS)], axis=0)
 
-    def values(start, stop):
-        @pl.loop(start, stop)
+    def values(half):
+        @pl.loop(0, count)
         def _(chunk):
             for h in range(TP):
-                weights = score[h, chunk_rows(chunk)]
-                acc = total[heads(h)]
+                weights = score[h, chunk_rows(chunk), half]
+                acc = total[heads(h), half]
                 for i in range(SLOTS):
-                    acc = acc + vc[chunk * SLOTS + i, h].astype(F32) * weights[i:i + 1]
-                total[heads(h)] = acc
+                    acc = acc + vc[chunk * SLOTS + i, h, :, half].astype(F32) * weights[i:i + 1]
+                total[heads(h), half] = acc
+
+    def after_first(rows, total_rows):
+        x1[rows] = (hid[rows].astype(F32) + total_rows.astype(F32)).astype(BF16)
+
+    def after_second(rows, total_rows):
+        out[rows] = (x1[rows].astype(F32) + total_rows.astype(F32)).astype(BF16)
+
+    line1 = _LineSum(part, inbox, mid, cross, send1, recv1, after_first)
+    line2 = _LineSum(part2, inbox2, mid2, cross2, send2, recv2, after_second)
+
+    def attend(index):
+        half = slice(LANES * index, LANES * (index + 1))
+        slot = _sublane((kc.shape[0], LANES))
+        lens_half = lens_row[:, half]
+        for h in range(TP):
+            fresh = jnp.sum(kt[heads(h), half].astype(F32) * qt[heads(h), half], axis=0, keepdims=True)
+            raw = jnp.where(slot == lens_half, fresh, score[h, :, half]) * (HEAD ** -0.5)
+            raw = jnp.where(slot <= lens_half, raw, -1e30)
+            weight = jnp.exp(raw - jnp.max(raw, axis=0, keepdims=True))
+            weight = (weight / jnp.sum(weight, axis=0, keepdims=True)).astype(BF16).astype(F32)
+            newest = jnp.sum(jnp.where(slot == lens_half, weight, 0.0), axis=0, keepdims=True)
+            score[h, :, half] = jnp.where(slot == lens_half, 0.0, weight)
+            total[heads(h), half] = vt[heads(h), half].astype(F32) * newest
+        values(half)
+        part[half] = _dot(total[:, half].T.astype(BF16), oo[...], 1, 1).astype(BF16)
+        for k in range(CHUNKS // 2 * index, CHUNKS // 2 * (index + 1)):
+            line1.push(k)
 
     count = kc.shape[0] // SLOTS
     scores(0, count // 2)
+    spreads[OUT].third()
+    spreads[DOWN].second()
+    scores(count // 2, count)
+    spreads[V].last()
+    vt[...] = project(ov, V)
     got_root(UP)
     spreads[UP].first()
-    scores(count // 2, count)
+    spreads[OUT].last()
+    attend(0)
+    attend(1)
     spreads[GATE].second()
-    slot = _sublane((kc.shape[0], QUARTER))
-    for h in range(TP):
-        fresh = jnp.sum(kt[heads(h)].astype(F32) * qt[heads(h)], axis=0, keepdims=True)
-        raw = jnp.where(slot == lens_row, fresh, score[h]) * (HEAD ** -0.5)
-        raw = jnp.where(slot <= lens_row, raw, -1e30)
-        weight = jnp.exp(raw - jnp.max(raw, axis=0, keepdims=True))
-        weight = (weight / jnp.sum(weight, axis=0, keepdims=True)).astype(BF16).astype(F32)
-        newest = jnp.sum(jnp.where(slot == lens_row, weight, 0.0), axis=0, keepdims=True)
-        score[h] = jnp.where(slot == lens_row, 0.0, weight)
-        total[heads(h)] = vt[heads(h)].astype(F32) * newest
-    values(0, count // 2)
-    got_root(DOWN)
-    spreads[DOWN].first()
-    values(count // 2, count)
-    attended[...] = total[...].T.astype(BF16)
-    spreads[UP].second()
-    spreads[OUT].last()
-
-    def after_first(rows, total_rows):
-        x1[rows] = (hid[rows].astype(F32) + total_rows.astype(F32)).astype(BF16)
-
-    def after_second(rows, total_rows):
-        out[rows] = (x1[rows].astype(F32) + total_rows.astype(F32)).astype(BF16)
-
-    line1 = _LineSum(part, inbox, mid, cross, send1, recv1, after_first)
-    line2 = _LineSum(part2, inbox2, mid2, cross2, send2, recv2, after_second)
-
-    for half in range(2):
-        rows = pl.ds(LANES * half, LANES)
-        part[rows] = _dot(attended[rows], oo[...], 1, 1).astype(BF16)
-        for k in range(CHUNKS // 2 * half, CHUNKS // 2 * (half + 1)):
-            line1.push(k)
-    spreads[GATE].third()
-    spreads[DOWN].second()
-    spreads[UP].third()
+
+    lens_b = lens_row.astype(F32).astype(BF16)
+
+    def update(cache, new):
+        @pl.loop(0, kc.shape[0])
+        def _(slot):
+            here = lens_b == slot.astype(F32).astype(BF16)
+            for h in range(TP):
+                cache[slot, h] = jnp.where(here, new[heads(h)], cache[slot, h])
+
+    update(kc, kt)
+    spreads[DOWN].third()
 
     def mlp(block):
         size = BLOCK_CHUNKS * CHUNK
@@ -496,7 +517,7 @@
         gate = _dot(norm, og[...], 1, 1).astype(BF16).astype(F32)
         up = _dot(norm, ou[...], 1, 1).astype(BF16).astype(F32)
         gated = (jax.nn.silu(gate) * up).astype(BF16)
-        part2[rows] = _dot(gated, od[:, :FF], 1, 1).astype(BF16)
+        part2[rows] = _dot(gated, down[:, :FF], 1, 1).astype(BF16)
         for k in range(block * BLOCK_CHUNKS, (block + 1) * BLOCK_CHUNKS):
             line2.push(k)
 
@@ -507,17 +528,27 @@
                 spreads[w].last()
         if (k + 1) % BLOCK_CHUNKS == 0:
             mlp(k // BLOCK_CHUNKS)
+        if k == CHUNKS - 1 - BLOCK_CHUNKS:
+            for early in range(BLOCK_CHUNKS):
+                line2.join(early)
 
     for k in range(CHUNKS):
         line1.join(k)
+        if k == 0:
+            spreads[UP].second()
+        if k == 1:
+            update(vc, vt)
+            spreads[GATE].third()
         if k == LAG:
-            spreads[DOWN].third()
+            spreads[UP].third()
         if k >= LAG:
             finish_first(k - LAG)
     for k in range(CHUNKS - LAG, CHUNKS):
         finish_first(k)
-    for k in range(CHUNKS):
+    for k in range(BLOCK_CHUNKS, CHUNKS):
         line2.join(k)
+        if k == CHUNKS - 1:
+            od[...] = down[...].T[:FF]
         if k >= LAG:
             line2.finish(k - LAG)
     for k in range(CHUNKS - LAG, CHUNKS):
@@ -533,16 +564,17 @@
             copy.wait_send()
     for spread in spreads:
         spread.drain()
-    _remote(landed, landed, aux_send, aux_recv, z, peers["x"]).wait_send()
+    for index, size in enumerate((3, TP, 2 * TP, 4 * TP)):
+        board_got(index, size, True)
 
 
 def _step(weights, vectors, hid, lens, kc, vc):
     vmem = pl.BlockSpec(memory_space=pltpu.VMEM)
     anywhere = pl.BlockSpec(memory_space=pltpu.HBM)
     square = (QUARTER, QUARTER)
-    sizes = [(QUARTER, WIDTH)] * 3 + [(WIDTH, QUARTER), (WIDTH, FF_PAD)] + [(FF, WIDTH)] * 2
-    sizes += [square] * 2 + [(1, QUARTER)] * 3 + [(1, WIDTH)] * 2 + [kc.shape, vc.shape]
-    outs = [pltpu.VMEM(size, BF16) for size in sizes] + [pltpu.VMEM(lens.shape, lens.dtype), pltpu.VMEM(hid.shape, BF16)]
+    sizes = [(QUARTER, WIDTH)] * 3 + [(WIDTH, QUARTER)] + [(FF, WIDTH)] * 3
+    sizes += [(QUARTER,)] * 3 + [(WIDTH,)] * 2 + [kc.shape, vc.shape, hid.shape]
+    outs = [pltpu.VMEM(size, BF16) for size in sizes]
     dma = pltpu.SemaphoreType.DMA
     inputs = [_in_hbm(a) for a in (*weights, *vectors, hid, lens, kc, vc)]
     rows = pltpu.VMEM(hid.shape, BF16)
@@ -554,93 +586,50 @@
         scratch_shapes=[pltpu.VMEM(w.shape, BF16) for w in weights]
         + [pltpu.VMEM((4, weights[w].shape[0], QUARTER), BF16) for w in ROW_SHARED] + [
             pltpu.VMEM((TP, BLOCK, FF_PAD), BF16), pltpu.VMEM((5, 1, BLOCK), BF16), rows,
+            pltpu.VMEM(lens.shape, lens.dtype), pltpu.VMEM(square, BF16), pltpu.VMEM(square, BF16),
             pltpu.VMEM((2, 1, LANES), F32), pltpu.VMEM((TP * DP, 2, 1, LANES), F32), rows, pltpu.VMEM(square, F32),
-            pltpu.VMEM((TP, kc.shape[0], QUARTER), F32), pltpu.VMEM(square, F32), pltpu.VMEM(square, BF16)]
+            pltpu.VMEM((TP, kc.shape[0], QUARTER), F32), pltpu.VMEM(square, F32),
+            pltpu.VMEM((WIDTH, FF_PAD), BF16)]
         + [rows] * 9 + [
             dma((11,)), dma((5,)), dma((7,)), dma((7, 4)), dma((7, 4)), dma((7, 4)), dma((7,)),
-            dma((7, SPREAD_SENDS)), dma((7, SPREAD_RECVS)), dma, dma] + [dma((2, CHUNKS))] * 4,
+            dma((7, SPREAD_SENDS)), dma((7, SPREAD_RECVS)), dma((4,)), dma((4,))] + [dma((2, CHUNKS))] * 4,
         compiler_params=pltpu.CompilerParams(collective_id=0, has_side_effects=True, vmem_limit_bytes=24 * MIB),
         cost_estimate=pl.CostEstimate(flops=2 * 10**10, bytes_accessed=MIB, transcendentals=0),
         name="step",
     )(*inputs)
 
 
-BUFFERS = 4
-
-
 def _emit_kernel(*refs):
-    kc, vc, kn, vn, lens, down = refs[:6]
-    plain = refs[6:13]
-    vectors = refs[13:18]
-    ko, vo, od = refs[18:21]
-    plain_out = refs[21:28]
-    vectors_out = refs[28:33]
-    stage, turned, sem, pass_sem, down_sem = refs[33:]
-
-    passing = [pltpu.make_async_copy(src, dst, pass_sem.at[i]) for i, (src, dst) in enumerate(zip(plain, plain_out))]
-    for copy in passing:
+    count = len(refs) // 2
+    copies = [pltpu.make_async_copy(refs[i], refs[count + i], refs[-1].at[i]) for i in range(count)]
+    for copy in copies:
         copy.start()
-    for src, dst in zip(vectors, vectors_out):
-        dst[...] = src[...].reshape(dst.shape)
-
-    lens_b = lens[...].astype(F32).astype(BF16)
-    count = kc.shape[0] // SLOTS
-
-    def put(dst, index, chunk):
-        return pltpu.make_async_copy(stage.at[index], dst.at[pl.ds(chunk * SLOTS, SLOTS)], sem.at[index])
-
-    def update(old, new, dst, first):
-        @pl.loop(0, count)
-        def _(chunk):
-            index = (chunk + first) % BUFFERS
-
-            @pl.when(chunk + first >= BUFFERS)
-            def _():
-                put(dst, index, 0).wait()
-
-            for i in range(SLOTS):
-                slot = chunk * SLOTS + i
-                here = lens_b == slot.astype(F32).astype(BF16)
-                for h in range(TP):
-                    stage[index, i, h] = jnp.where(here, new[HEAD * h:HEAD * (h + 1)], old[slot, h])
-            put(dst, index, chunk).start()
-
-    update(kc, kn, ko, 0)
-    turned[...] = down[...].T
-    turn = pltpu.make_async_copy(turned.at[pl.ds(0, FF)], od, down_sem)
-    turn.start()
-    update(vc, vn, vo, count)
-    for index in range(BUFFERS):
-        put(vo, index, 0).wait()
-    for copy in passing + [turn]:
+    for copy in copies:
         copy.wait()
 
 
-def _emit(kc, vc, kn, vn, lens, down, plain, vectors):
+def _emit(arrays):
     vmem, hbm = pl.BlockSpec(memory_space=pltpu.VMEM), pl.BlockSpec(memory_space=pltpu.HBM)
-    shapes = [kc.shape, vc.shape, (FF, WIDTH)] + [a.shape for a in plain] + [(v.size,) for v in vectors]
-    dma = pltpu.SemaphoreType.DMA
     return pl.pallas_call(
         _emit_kernel,
-        out_shape=[jax.ShapeDtypeStruct(shape, BF16) for shape in shapes],
-        in_specs=[vmem] * (6 + len(plain) + len(vectors)),
-        out_specs=[hbm] * (3 + len(plain)) + [vmem] * len(vectors),
-        scratch_shapes=[pltpu.VMEM((BUFFERS, SLOTS) + kc.shape[1:], BF16), pltpu.VMEM((FF_PAD, WIDTH), BF16),
-                        dma((BUFFERS,)), dma((len(plain),)), dma],
-        compiler_params=pltpu.CompilerParams(vmem_limit_bytes=12 * MIB),
+        out_shape=[jax.ShapeDtypeStruct(a.shape, BF16) for a in arrays],
+        in_specs=[vmem] * len(arrays),
+        out_specs=[hbm] * len(arrays),
+        scratch_shapes=[pltpu.SemaphoreType.DMA((len(arrays),))],
+        compiler_params=pltpu.CompilerParams(vmem_limit_bytes=4 * MIB),
         cost_estimate=pl.CostEstimate(flops=10**9, bytes_accessed=24 * MIB, transcendentals=0),
         name="emit",
-    )(kc, vc, kn, vn, lens, down, *plain, *vectors)
+    )(*arrays)
 
 
 def solution(mesh):
     def local_step(wq, bq, wk, bk, wv, bv, wo, wg, wu, wd, ga, gm, hid, k_cache, v_cache, lengths):
         vectors = [v.reshape(1, -1) for v in (bq, bk, bv, ga, gm)]
         kc, vc = jnp.transpose(k_cache, (1, 2, 3, 0)), jnp.transpose(v_cache, (1, 2, 3, 0))
-        (gq, gk, gv, go, gd, gg, gu, kt, vt, gbq, gbk, gbv, gga, ggm, kc_v, vc_v, lens_v, out_v) = _step(
+        (gq, gk, gv, go, gd, gg, gu, gbq, gbk, gbv, gga, ggm, kc_v, vc_v, out_v) = _step(
             (wq, wk, wv, wo, wd, wg, wu), vectors, hid, lengths.reshape(1, -1), kc, vc)
-        ko, vo, od, oq, ok, ov, oo, og, ou, out, obq, obk, obv, oga, ogm = _emit(
-            kc_v, vc_v, kt, vt, lens_v, gd, (gq, gk, gv, go, gg, gu, out_v), (gbq, gbk, gbv, gga, ggm))
+        ko, vo, og, ou, od, oq, ok, ov, oo, out, obq, obk, obv, oga, ogm = _emit(
+            (kc_v, vc_v, gg, gu, gd, gq, gk, gv, go, out_v, gbq, gbk, gbv, gga, ggm))
         return (oq, obq, ok, obk, ov, obv, oo, og, ou, od.T, oga, ogm, out,
                 jnp.transpose(ko, (3, 0, 1, 2)), jnp.transpose(vo, (3, 0, 1, 2)))
 

time: 86.9 us -> 79.2 us (0.911)
  Pallas kernels: 86 us -> 78.3 us
    pallas_call x1, Pallas kernels: 77.4 us -> 70.2 us  [_step(): pl.pallas_call(_step_kernel, out_shape=outs, in_specs=[anywhere] * len(in...]
where the time goes in v3:
time: 79.2 us; the launch traced here: 79 us
  Pallas kernels  78.3 us (99%)
    pallas_call x1, Pallas kernels, _step(): pl.pallas_call(_step_kernel, out_shape=outs, in_specs=[anywhere] * len(in...  70.2 us
    pallas_call x1, Pallas kernels, _emit(): pl.pallas_call(_emit_kernel, out_shape=[jax.ShapeDtypeStruct(a.shape, BF1...  8.17 us

profile of v3, /device:TPU:0, one launch (start us, length us, event | category | flops | bytes accessed | tf_op | source)
XLA Modules:
  0.0 79.0 jit_solution(13334746433418521134)
XLA Ops:
  0.7 70.2 %step.1 = (bf16[256,1024]{1,0:T(8,128)(2,1)S(1)}, bf16[256,1024]{1,0:T(8,128)(2,1)S(1)}, bf16[256,1024]{1,0:T(8,128)(2,1)S(1)}, bf16[1024,256]{1,0:T(8,128)(2,1)...) custom-call(bf16[32,1024]{1,0:T(8,128)(2,1)} %wq.1, ...), custom_call_target="tpu_custom_call" | custom-call | flops 20000000000 | bytes 1048576 | tf_op jit(solution)/shard_map/step/pallas_call | solution.py:581
  70.8 8.2 %emit.1 = (bf16[64,4,64,256]{3,2,1,0:T(8,128)(2,1)}, bf16[64,4,64,256]{3,2,1,0:T(8,128)(2,1)}, bf16[704,1024]{1,0:T(8,128)(2,1)}, bf16[704,1024]{1,0:T(8,128)(2,...) custom-call(bf16[64,4,64,256]{3,2,1,0:T(8,128)(2,1)S(1)} %get-tuple-, ...), custom_call_target="tpu_custom_call" | custom-call | flops 1000000000 | bytes 25165824 | tf_op jit(solution)/shard_map/emit/pallas_call | solution.py:613

commit v4 on v3

--- a/solution.py
+++ b/solution.py
@@ -410,6 +410,7 @@
     got_root(DOWN)
     spreads[DOWN].first()
     spreads[K].third()
+    spreads[V].third()
 
     def project(weight, r):
         return (_dot(weight[...], act[...], 1, 1) + bias_column(r)).astype(BF16)
@@ -424,7 +425,6 @@
 
     spreads[Q].last()
     rotate(project(oq, Q), qt)
-    spreads[V].third()
     spreads[K].last()
     rotate(project(ok, K), kt)
     got_root(GATE)

time: 79.2 us -> 78.7 us (level)
  no operation moved by 1% of the time
where the time goes in v4:
time: 78.7 us; the launch traced here: 78.6 us
  Pallas kernels  77.9 us (99%)
    pallas_call x1, Pallas kernels, _step(): pl.pallas_call(_step_kernel, out_shape=outs, in_specs=[anywhere] * len(in...  69.7 us
    pallas_call x1, Pallas kernels, _emit(): pl.pallas_call(_emit_kernel, out_shape=[jax.ShapeDtypeStruct(a.shape, BF1...  8.17 us

profile of v4, /device:TPU:0, one launch (start us, length us, event | category | flops | bytes accessed | tf_op | source)
XLA Modules:
  0.0 78.6 jit_solution(16141616188735663260)
XLA Ops:
  0.7 69.7 %step.1 = (bf16[256,1024]{1,0:T(8,128)(2,1)S(1)}, bf16[256,1024]{1,0:T(8,128)(2,1)S(1)}, bf16[256,1024]{1,0:T(8,128)(2,1)S(1)}, bf16[1024,256]{1,0:T(8,128)(2,1)...) custom-call(bf16[32,1024]{1,0:T(8,128)(2,1)} %wq.1, ...), custom_call_target="tpu_custom_call" | custom-call | flops 20000000000 | bytes 1048576 | tf_op jit(solution)/shard_map/step/pallas_call | solution.py:581
  70.4 8.2 %emit.1 = (bf16[64,4,64,256]{3,2,1,0:T(8,128)(2,1)}, bf16[64,4,64,256]{3,2,1,0:T(8,128)(2,1)}, bf16[704,1024]{1,0:T(8,128)(2,1)}, bf16[704,1024]{1,0:T(8,128)(2,...) custom-call(bf16[64,4,64,256]{3,2,1,0:T(8,128)(2,1)S(1)} %get-tuple-, ...), custom_call_target="tpu_custom_call" | custom-call | flops 1000000000 | bytes 25165824 | tf_op jit(solution)/shard_map/emit/pallas_call | solution.py:613
